TPU v7x, 32 devices: a whole 2x2x4 slice. The times are simulated.
32 devices in a mesh: dp: 16 (over z, x, core), seq: 2 (over y).
Axes of the slice: x: 2, y: 2, z: 4, core: 2. Of those that a mesh axis runs over, the one named last changes fastest.
Arguments:
- frames: bfloat16 [16, 1024, 512], P('dp', 'seq'), may hold values from -6 to 6
- cotangent: bfloat16 [16, 1024, 512], P('dp', 'seq'), may hold values from -6 to 6
- weight_in: bfloat16 [2, 512, 2176], replicated, may hold values from -0.25 to 0.25
- qk_scales: float32 [2, 2, 128], replicated, may hold values from 0.5 to 1.5
- weight_out: bfloat16 [2, 1024, 512], replicated, may hold values from -0.1875 to 0.1875
- gains: float32 [2, 512], replicated, may hold values from 0.5 to 1.5
Outputs:
- output: bfloat16 [16, 1024, 512], P('dp', 'seq')
- grad_frames: bfloat16 [16, 1024, 512], P('dp', 'seq')
- grad_in: float32 [2, 512, 2176], P(None, 'dp')
- grad_out: float32 [2, 1024, 512], P(None, 'dp')
- grad_gains: float32 [2, 512], replicated
- grad_scales: float32 [2, 2, 128], replicated
All inputs are finite; a program needn't handle non-finite values.
Results may differ from a plain program's by a relative error of at most 0.028.
Values may be sent and summed in bfloat16 or wider, within the bound.
No kernel may reach another device: no remote copies, remote signals or barrier semaphores. Data moves between devices by JAX's collectives and lax.ppermute only.
A program may use at most 192 MiB of HBM per device.

v0:
```python
from functools import partial

import jax
import jax.numpy as jnp
from jax import lax
from jax.experimental import pallas as pl
from jax.experimental.pallas import tpu as pltpu
from jax.sharding import PartitionSpec as P


BLOCK = 256


EPSILON = 1e-06


def sigmoid(values):
    return 0.5 * jnp.tanh(0.5 * values) + 0.5


def slope(values, sig):
    return sig * (1.0 + values * (1.0 - sig))


def dot(left, right, left_dim=1, right_dim=0):
    return lax.dot_general(
        left, right, (((left_dim,), (right_dim,)), ((), ())), preferred_element_type=jnp.float32
    )


def column_chunks(total, size):
    return [(at, min(size, total - at)) for at in range(0, total, size)]


CHUNK = 256


def norm_parts(values):
    scaling = lax.rsqrt(jnp.mean(values * values, axis=-1, keepdims=True) + EPSILON)
    return scaling, values * scaling


def norm_back(values, upstream, grad_hidden, gain_row):
    scaling, unit = norm_parts(values)
    grad_gain = jnp.sum(grad_hidden * unit, axis=0, keepdims=True)
    scaled = grad_hidden * gain_row
    mean = jnp.mean(scaled * unit, axis=-1, keepdims=True)
    return upstream + scaling * (scaled - unit * mean), grad_gain


def group_mask(rows, columns, positions):
    left = lax.broadcasted_iota(jnp.int32, (rows, columns), 0)
    right = lax.broadcasted_iota(jnp.int32, (rows, columns), 1)
    return lax.rem(left, positions) == lax.rem(right, positions)


def scores_of(query, keyed, positions):
    found = jnp.maximum(dot(query, keyed, 1, 1) * query.shape[1] ** (-0.5), 0.0)
    if positions is not None:
        found = jnp.where(group_mask(found.shape[0], found.shape[1], positions), found, 0.0)
    return found


def forward_core(x_ref, h_ref, p_ref, v_ref, o_ref, g_ref, r_ref, win, wout, scales, gain, sets, positions, length):
    half = wout.shape[0]
    values = x_ref[...].astype(jnp.float32)
    h_ref[...] = (norm_parts(values)[1] * gain[...]).astype(jnp.bfloat16)
    shared = dot(h_ref[...], win[:, 2 * half :])
    p_ref[:, 2 * half :] = shared.astype(p_ref.dtype)
    active = shared * sigmoid(shared)
    query = (active * scales[0:1, :]).astype(jnp.bfloat16)
    keyed = (active * scales[1:2, :]).astype(jnp.bfloat16)
    weights = []
    for start, stop in sets:
        found = scores_of(query[start:stop], keyed[start:stop], positions)
        if r_ref is not None:
            r_ref[start:stop, :] = found
        weights.append((found * found * (1.0 / length)).astype(jnp.bfloat16))
    for at, size in column_chunks(half, CHUNK):
        value = dot(h_ref[...], win[:, half + at : half + at + size])
        p_ref[:, half + at : half + at + size] = value.astype(p_ref.dtype)
        v_ref[:, at : at + size] = (value * sigmoid(value)).astype(jnp.bfloat16)
        gate = dot(h_ref[...], win[:, at : at + size])
        p_ref[:, at : at + size] = gate.astype(p_ref.dtype)
        gate = gate * sigmoid(gate)
        for (start, stop), weight in zip(sets, weights):
            mixed = dot(weight, v_ref[start:stop, at : at + size])
            if o_ref is not None:
                o_ref[start:stop, at : at + size] = mixed
            g_ref[start:stop, at : at + size] = (gate[start:stop] * mixed).astype(jnp.bfloat16)
    return values + dot(g_ref[...], wout[...])


def backward_core(dr_ref, p_ref, v_ref, o_ref, g_ref, r_ref, do_ref, dp_ref, wout, scales, sets, positions, length):
    half = wout.shape[0]
    width = scales.shape[1]
    again = o_ref is None
    shared = p_ref[:, 2 * half :].astype(jnp.float32)
    shared_sig = sigmoid(shared)
    active = shared * shared_sig
    query = (active * scales[0:1, :]).astype(jnp.bfloat16)
    keyed = (active * scales[1:2, :]).astype(jnp.bfloat16)
    found, weights = [], []
    for start, stop in sets:
        if again:
            found.append(scores_of(query[start:stop], keyed[start:stop], positions))
        else:
            found.append(r_ref[start:stop, :])
        weights.append((found[-1] * found[-1] * (1.0 / length)).astype(jnp.bfloat16))
    grad_weights = [None for _ in sets]
    for at, size in column_chunks(half, CHUNK):
        here = slice(at, at + size)
        value_here = slice(half + at, half + at + size)
        value = p_ref[:, value_here].astype(jnp.float32)
        value_sig = sigmoid(value)
        if again:
            v_ref[:, here] = (value * value_sig).astype(jnp.bfloat16)
        grad_gated = dot(dr_ref[...], wout[here, :], 1, 1).astype(jnp.bfloat16).astype(jnp.float32)
        gate = p_ref[:, here].astype(jnp.float32)
        gate_sig = sigmoid(gate)
        gated = gate * gate_sig
        do_ref[:, here] = (grad_gated * gated).astype(jnp.bfloat16)
        outer = grad_gated * slope(gate, gate_sig)
        inner = slope(value, value_sig)
        for index, (start, stop) in enumerate(sets):
            if again:
                mixed = dot(weights[index], v_ref[start:stop, here])
                g_ref[start:stop, here] = (gated[start:stop] * mixed).astype(jnp.bfloat16)
            else:
                mixed = o_ref[start:stop, here]
            dp_ref[start:stop, here] = (outer[start:stop] * mixed).astype(jnp.bfloat16)
            grad_value = dot(weights[index], do_ref[start:stop, here], 0, 0)
            grad_value = grad_value.astype(jnp.bfloat16).astype(jnp.float32)
            dp_ref[start:stop, value_here] = (grad_value * inner[start:stop]).astype(jnp.bfloat16)
    totals = [jnp.zeros((1, width), jnp.float32), jnp.zeros((1, width), jnp.float32)]
    for index, (start, stop) in enumerate(sets):
        grad_weight = dot(do_ref[start:stop, :], v_ref[start:stop, :], 1, 1)
        grad_weight = grad_weight.astype(jnp.bfloat16).astype(jnp.float32)
        grad_score = grad_weight * found[index] * (2.0 / length * width ** (-0.5))
        if positions is not None:
            grad_score = jnp.where(
                group_mask(grad_score.shape[0], grad_score.shape[1], positions), grad_score, 0.0
            )
        grad_score = grad_score.astype(jnp.bfloat16)
        part = active[start:stop]
        grad_query = dot(grad_score, keyed[start:stop]).astype(jnp.bfloat16).astype(jnp.float32)
        grad_keyed = dot(grad_score, query[start:stop], 0, 0).astype(jnp.bfloat16).astype(jnp.float32)
        totals[0] += jnp.sum(grad_query * part, axis=0, keepdims=True)
        totals[1] += jnp.sum(grad_keyed * part, axis=0, keepdims=True)
        grad_shared = grad_query * scales[0:1, :] + grad_keyed * scales[1:2, :]
        grad_shared = grad_shared * slope(shared[start:stop], shared_sig[start:stop])
        dp_ref[start:stop, 2 * half :] = grad_shared.astype(jnp.bfloat16)
    return totals


def copy_blocks(shape, me, source, target):
    slots, blocks, positions = shape
    size = slots * positions
    for b in range(blocks):
        for k in range(slots):
            at = pl.multiple_of((me ^ k) * positions, positions)
            target[b * size + k * positions : b * size + (k + 1) * positions, :] = source[b, pl.ds(at, positions), :]


def first_kernel(shape, me_ref, frames, win, wout, scales, gain, *rest):
    slots, blocks, positions = shape
    sends, (h_ref, p_ref, x_ref, v_ref, g_ref) = rest[:slots], rest[slots:]
    size = slots * positions
    copy_blocks(shape, me_ref[0], frames.now(), x_ref)
    sets = [(b * size, (b + 1) * size) for b in range(blocks)]
    result = forward_core(
        x_ref, h_ref, p_ref, v_ref, None, g_ref, None, win, wout, scales, gain, sets, None, size
    ).astype(jnp.bfloat16)
    for b in range(blocks):
        for k in range(slots):
            sends[k][b * positions : (b + 1) * positions, :] = result[b * size + k * positions : b * size + (k + 1) * positions]


def second_kernel(shape, length, scaling, me_ref, cotangent, win, wout, scales, gain, *rest):
    slots, blocks, positions = shape
    part = blocks * positions
    xs, drs, rest = rest[:slots], rest[slots : 2 * slots - 1], rest[2 * slots - 1 :]
    seconds, backs, rest = rest[:slots], rest[slots : 2 * slots], rest[2 * slots :]
    h_ref, dp_ref, g_ref, dr_ref, small, x_ref, p_ref, v_ref, o_ref, r_ref, do_ref = rest
    at = pl.multiple_of(me_ref[0] * positions, positions)
    for k in range(slots):
        x_ref[k * part : (k + 1) * part, :] = xs[k][...]
        if k:
            dr_ref[k * part : (k + 1) * part, :] = drs[k - 1][...]
    for b in range(blocks):
        dr_ref[b * positions : (b + 1) * positions, :] = cotangent.now()[b, pl.ds(at, positions), :]
    sets = [(0, x_ref.shape[0])]
    result = forward_core(
        x_ref, h_ref, p_ref, v_ref, o_ref, g_ref, r_ref, win, wout, scales, gain, sets, positions, length
    ).astype(jnp.bfloat16)
    for k in range(slots):
        seconds[k][...] = result[k * part : (k + 1) * part]
    totals = backward_core(
        dr_ref, p_ref, v_ref, o_ref, g_ref, r_ref, do_ref, dp_ref, wout, scales, sets, positions, length
    )
    grad_hidden = dot(dp_ref[...], win[...], 1, 1)
    result, grad_gain = norm_back(
        x_ref[...].astype(jnp.float32), dr_ref[...].astype(jnp.float32), grad_hidden, gain[...]
    )
    result = result.astype(jnp.bfloat16)
    for k in range(slots):
        backs[k][...] = result[k * part : (k + 1) * part]
    fill_small(small, 0, scaling, [grad_gain] + totals)


def fill_small(small, start, scaling, values):
    row = start
    for value in values:
        for at in range(0, value.shape[1], 128):
            small[row : row + 1, :] = value[:, at : at + 128] * scaling
            row += 1
    while row % 8:
        small[row : row + 1, :] = jnp.zeros((1, 128), jnp.float32)
        row += 1


def third_kernel(shape, wout, scales, *rest):
    slots, blocks, positions = shape
    size = slots * positions
    slot_refs, (p_ref, dr_ref, dp_ref, g_ref, dscales, v_ref, do_ref) = rest[:slots], rest[slots:]
    for b in range(blocks):
        for k in range(slots):
            dr_ref[b * size + k * positions : b * size + (k + 1) * positions, :] = slot_refs[k][b * positions : (b + 1) * positions, :]
    sets = [(b * size, (b + 1) * size) for b in range(blocks)]
    totals = backward_core(
        dr_ref, p_ref, v_ref, None, g_ref, None, do_ref, dp_ref, wout, scales, sets, None, size
    )
    dscales[0:1, :] = totals[0]
    dscales[1:2, :] = totals[1]


def fourth_kernel(shape, scaling, me_ref, frames, win, gain, dr_ref, dp_ref, dscales, late_small, *rest):
    slots, blocks, positions = shape
    slot_refs, (grad_frames, output, small, x_ref) = rest[:slots], rest[slots:]
    me = me_ref[0]
    size = slots * positions
    copy_blocks(shape, me, frames.now(), x_ref)
    for b in range(blocks):
        for k in range(slots):
            at = pl.multiple_of((me ^ k) * positions, positions)
            output[b, pl.ds(at, positions), :] = slot_refs[k][b * positions : (b + 1) * positions, :]
    grad_hidden = dot(dp_ref[...], win[...], 1, 1)
    result, grad_gain = norm_back(
        x_ref[...].astype(jnp.float32), dr_ref[...].astype(jnp.float32), grad_hidden, gain[...]
    )
    result = result.astype(jnp.bfloat16)
    for b in range(blocks):
        for k in range(slots):
            at = pl.multiple_of((me ^ k) * positions, positions)
            grad_frames[b, pl.ds(at, positions), :] = result[b * size + k * positions : b * size + (k + 1) * positions]
    fill_small(small, 0, scaling, [grad_gain, dscales[0:1, :], dscales[1:2, :]])
    half = late_small.shape[0]
    small[half:, :] = late_small[...]


def weights_kernel(plan, shards, scaling, me_ref, h_ref, dp_ref, g_ref, dr_ref, *rest):
    outs, (buffer,) = rest[: 2 * len(plan)], rest[2 * len(plan) :]
    me = me_ref[0]
    rows = outs[0].shape[1]
    width = dp_ref.shape[1]

    def place(index, column, size, offset_of):
        _, _, offsets = plan[index]
        kept, away = outs[2 * index], outs[2 * index + 1]
        for at, offset in enumerate(offsets):
            target = kept if at < shards // 2 else away
            top = pl.multiple_of(offset_of(me ^ offset), rows)
            target[at % (shards // 2), :, column : column + size] = buffer[pl.ds(top, rows), 0:size]

    count = buffer.shape[1]
    for index, (start, stop, _) in enumerate(plan):
        for at, size in column_chunks(max(min(stop, width) - start, 0), count):
            found = dot(h_ref[...], dp_ref[:, start + at : start + at + size], 0, 0) * scaling
            buffer[0 : h_ref.shape[1], 0:size] = found.astype(jnp.bfloat16)
            place(index, at, size, lambda r: r * rows)
    per = dr_ref.shape[1]
    pieces = g_ref.shape[1] // (shards * rows)
    for at, size in column_chunks(per, count):
        buffer[:, 0:size] = (dot(g_ref[...], dr_ref[:, at : at + size], 0, 0) * scaling).astype(jnp.bfloat16)
        for index, (start, stop, _) in enumerate(plan):
            for k in range(pieces):
                if start <= width + k * per + at < stop:
                    place(index, width + k * per + at - start, size, lambda r, k=k: (r * pieces + k) * rows)


def last_kernel(plans, small_ref, small_came, *rest):
    count = sum(len(plan) for plan in plans)
    parts, (grad_in, grad_out, gains, scales) = rest[: 2 * count], rest[2 * count :]
    width, per = grad_in.shape[2], grad_out.shape[2]
    rows = grad_in.shape[1]
    at = 0
    for unit, plan in enumerate(plans):
        for start, stop, _ in plan:
            kept, came = parts[2 * at], parts[2 * at + 1]
            at += 1
            total = kept[0].astype(jnp.float32) + came[0].astype(jnp.float32)
            low = min(stop, width)
            if start < low:
                grad_in[unit, :, start:low] = total[:, : low - start]
            for k in range(grad_out.shape[1] // rows):
                left, right = max(start, width + k * per), min(stop, width + (k + 1) * per)
                if left < right:
                    grad_out[unit, k * rows : (k + 1) * rows, left - width - k * per : right - width - k * per] = total[:, left - start : right - start]
    total = small_ref[...] + small_came[...]
    half = total.shape[0] // 2
    for unit in range(2):
        row = unit * half
        for column in range(0, gains.shape[1], 128):
            gains[unit : unit + 1, column : column + 128] = total[row : row + 1, :]
            row += 1
        for which in range(2):
            for column in range(0, scales.shape[2], 128):
                scales[unit, which : which + 1, column : column + 128] = total[row : row + 1, :]
                row += 1


VMEM = pltpu.MemorySpace.VMEM
SMEM = pltpu.MemorySpace.SMEM
HBM = pltpu.MemorySpace.HBM
LIMIT = 28 * 2**20


class Fetched:
    def __init__(self, source, unit, target, semaphore):
        self.copy = pltpu.make_async_copy(source if unit is None else source.at[unit], target, semaphore)
        self.copy.start()
        self.target = target
        self.shape = target.shape
        self.landed = False

    def now(self):
        if not self.landed:
            self.copy.wait()
            self.landed = True
        return self.target

    def __getitem__(self, index):
        return self.now()[index]


def run(body, ins, outs, scratch, flops):
    kinds = [len(v) if isinstance(v, tuple) else 0 for v in ins]
    fetched = [i for i, kind in enumerate(kinds) if kind == 2]
    specs = [pl.BlockSpec(memory_space=(VMEM, SMEM, HBM)[kind]) for kind in kinds]
    targets = []
    for i in fetched:
        array, unit = ins[i]
        targets.append(pltpu.VMEM(array.shape if unit is None else array.shape[1:], array.dtype))

    def kernel(*refs):
        refs = list(refs)
        spare = refs[len(refs) - len(fetched) - 1 :] if fetched else []
        refs = refs[: len(refs) - len(spare)]
        for k, i in enumerate(fetched):
            refs[i] = Fetched(refs[i], ins[i][1], spare[k], spare[-1].at[k])
        body(*refs)

    return pl.pallas_call(
        kernel,
        out_shape=[jax.ShapeDtypeStruct(s, d) for s, d in outs],
        in_specs=specs,
        out_specs=[pl.BlockSpec(memory_space=VMEM) for _ in outs],
        scratch_shapes=[pltpu.VMEM(s, d) for s, d in scratch]
        + targets
        + ([pltpu.SemaphoreType.DMA((len(fetched),))] if fetched else []),
        compiler_params=pltpu.CompilerParams(vmem_limit_bytes=LIMIT),
        cost_estimate=pl.CostEstimate(flops=flops, bytes_accessed=2**22, transcendentals=0),
    )(*[v[0] if isinstance(v, tuple) else v for v in ins])


def swapped(values, axis, mask):
    return lax.ppermute(values, axis, [(i, i ^ mask) for i in range(lax.axis_size(axis))])


def masks_of(size):
    count = size.bit_length() - 1
    masks = [1 << b for b in range(count)]
    if count >= 3:
        masks[-1] |= masks[-2]
    return masks


def rotated(masks, turn):
    first, *rest = masks
    turn %= max(len(rest), 1)
    return [first] + rest[turn:] + rest[:turn]


def offsets_of(masks):
    count = len(masks)
    offsets = []
    for place in range(1 << count):
        mask = 0
        for step in range(count):
            if place >> (count - 1 - step) & 1:
                mask ^= masks[step]
        offsets.append(mask)
    return offsets


def plan_of(width, turns):
    masks = masks_of(lax.axis_size("dp"))
    edges = [width * k // len(turns) // 128 * 128 for k in range(len(turns))] + [width]
    return [(edges[k], edges[k + 1], offsets_of(rotated(masks, turn))) for k, turn in enumerate(turns)]


class Chain:
    def __init__(self, kept, away, turn):
        self.steps = [("dp", m) for m in rotated(masks_of(lax.axis_size("dp")), turn)]
        self.halvings = len(self.steps)
        self.steps += [("seq", m) for m in masks_of(lax.axis_size("seq"))]
        self.kept, self.away = kept, away
        self.at = 0

    def send(self):
        self.came = swapped(self.away, *self.steps[self.at])

    def land(self):
        self.at += 1
        if self.done():
            return
        kept = self.kept.astype(jnp.float32)
        came = self.came.astype(jnp.float32)
        if self.at < self.halvings:
            half = kept.shape[0] // 2
            self.away = (kept[half:] + came[half:]).astype(jnp.bfloat16)
            self.kept = (kept[:half] + came[:half]).astype(jnp.bfloat16)
        else:
            self.away = self.kept = (kept + came).astype(jnp.bfloat16)

    def done(self):
        return self.at == len(self.steps)


LATE = (2,)
EARLY = (0, 1)


def unit_chains(plan, turns, scaling, me, hidden, grad_proj, gated, grad_result):
    size = lax.axis_size("dp")
    rows = hidden.shape[1] // size
    outs = [((size // 2, rows, stop - start), jnp.bfloat16) for start, stop, _ in plan for _ in range(2)]
    buffers = run(
        partial(weights_kernel, plan, size, scaling),
        [(me,), hidden, grad_proj, gated, grad_result],
        outs,
        [((max(hidden.shape[1], gated.shape[1]), 512), jnp.bfloat16)],
        2 * hidden.shape[0] * size * rows * plan[-1][1],
    )
    return [Chain(buffers[2 * k], buffers[2 * k + 1], turn) for k, turn in enumerate(turns)]


def tied(*values):
    return lax.optimization_barrier(values)


def on_device(frames, cotangent, weight_in, qk_scales, weight_out, gains):
    slots = lax.axis_size("seq")
    blocks = frames.shape[1] // BLOCK
    positions = BLOCK // slots
    shape = (slots, blocks, positions)
    count, width = frames.shape[1:]
    part = blocks * positions
    inner, half, shared = weight_in.shape[2], weight_out.shape[1], qk_scales.shape[2]
    tokens_all = frames.shape[0] * count * lax.axis_size("dp") * slots
    scaling = tokens_all ** (-0.5)
    me = lax.axis_index("seq").astype(jnp.int32).reshape(1)
    own = lax.axis_index("dp").astype(jnp.int32).reshape(1)
    flops = 2 * count * width * inner
    bf16, f32 = jnp.bfloat16, jnp.float32
    blocked = frames.reshape(blocks, BLOCK, width)
    turned = cotangent.reshape(blocks, BLOCK, width)
    lines = -(-(width + 2 * shared) // 1024) * 8
    slot_outs = [((part, width), bf16) for _ in range(slots)]

    def exchange(sends):
        return [swapped(sends[k], "seq", k) for k in range(1, slots)]

    pieces = turned.reshape(blocks, slots, positions, width)
    upstream = exchange(
        [
            lax.dynamic_index_in_dim(pieces, me[0] ^ k, 1, keepdims=False).reshape(part, width) if k else None
            for k in range(slots)
        ],
    )
    *first, hidden_first, proj_first = run(
        lambda me, x, wi, wo, sc, ga, *rest: first_kernel(
            shape, me, x, wi, wo, sc, Row(ga, 0), *rest
        ),
        [(me,), (blocked, None), (weight_in, 0), (weight_out, 0), (qk_scales, 0), (gains, None)],
        slot_outs + [((count, width), bf16), ((count, inner), bf16)],
        [((count, width), bf16), ((count, half), bf16), ((count, half), bf16)],
        2 * flops,
    )
    first_came = exchange(first)
    results = run(
        lambda me, dr, wi, wo, sc, ga, *rest: second_kernel(
            shape, slots * blocks, scaling, me, dr, wi, wo, sc, Row(ga, 1), *rest
        ),
        [(me,), (turned, None), (weight_in, 1), (weight_out, 1), (qk_scales, 1), (gains, None)]
        + [first[0]] + first_came + upstream,
        slot_outs + slot_outs
        + [
            ((count, width), bf16),
            ((count, inner), bf16),
            ((count, half), bf16),
            ((count, width), bf16),
            ((lines, 128), f32),
        ],
        [
            ((count, width), bf16),
            ((count, inner), f32),
            ((count, half), bf16),
            ((count, half), f32),
            ((count, count), f32),
            ((count, half), bf16),
        ],
        4 * flops,
    )
    second, back = results[:slots], results[slots : 2 * slots]
    hidden_second, dproj_second, gated_second, dresult_second, late_small = results[2 * slots :]
    back_came = exchange(back)
    columns = inner + half * width // hidden_second.shape[1]
    plans = [plan_of(columns, EARLY), plan_of(columns, LATE)]
    late = unit_chains(plans[1], LATE, scaling, own, hidden_second, dproj_second, gated_second, dresult_second)
    for chain in late:
        chain.send()
        chain.land()
    for chain in late:
        chain.send()
    *second_sends, back_came[0] = tied(*second[1:], back_came[0])
    second_came = exchange([None] + second_sends)
    dresult, dproj_first, gated_first, dscale_early = run(
        lambda wo, sc, *rest: third_kernel(shape, wo, sc, *rest),
        [(weight_out, 0), (qk_scales, 0), back[0]] + back_came + [proj_first],
        [((count, width), bf16), ((count, inner), bf16), ((count, half), bf16), ((2, shared), f32)],
        [((count, half), bf16), ((count, half), bf16)],
        2 * flops,
    )
    early = unit_chains(plans[0], EARLY, scaling, own, hidden_first, dproj_first, gated_first, dresult)
    grad_frames, output, small = run(
        lambda me, x, wi, ga, *rest: fourth_kernel(shape, scaling, me, x, wi, Row(ga, 0), *rest),
        [(me,), (blocked, None), (weight_in, 0), (gains, None), dresult, dproj_first, dscale_early, late_small]
        + [second[0]] + second_came,
        [((blocks, BLOCK, width), bf16), ((blocks, BLOCK, width), bf16), ((2 * lines, 128), f32)],
        [((count, width), bf16)],
        flops,
    )
    for chain in early:
        chain.send()
    for chain in late + early:
        chain.land()
    masks = [(a, m) for a in ("dp", "seq") for m in masks_of(lax.axis_size(a))]
    small_at = 0
    while small_at < len(masks) or not all(c.done() for c in early + late):
        live = [c for c in early + late if not c.done()]
        if small_at and small_at < len(masks):
            small, *aways = tied(small, *[c.away for c in live])
        else:
            aways = tied(*[c.away for c in live])
        for chain, away in zip(live, aways):
            chain.away = away
            chain.send()
        if small_at < len(masks):
            small_came = swapped(small, *masks[small_at])
            small_at += 1
            if small_at < len(masks):
                small = small + small_came
        for chain in live:
            chain.land()
    grad_in, grad_out, grad_gains, grad_scales = run(
        partial(last_kernel, plans),
        [small, small_came] + [v for c in early + late for v in (c.kept, c.came)],
        [
            ((2, weight_in.shape[1] // lax.axis_size("dp"), inner), f32),
            ((2, half // lax.axis_size("dp"), width), f32),
            (gains.shape, f32),
            (qk_scales.shape, f32),
        ],
        [],
        1000,
    )
    return (
        output.reshape(frames.shape),
        grad_frames.reshape(frames.shape),
        grad_in,
        grad_out,
        grad_gains,
        grad_scales,
    )


class Row:
    def __init__(self, fetched, row):
        self.fetched, self.row = fetched, row

    def __getitem__(self, index):
        return self.fetched.now()[self.row : self.row + 1, :]


def solution(mesh):
    in_specs = (P("dp", "seq", None), P("dp", "seq", None), P(), P(), P(), P())
    out_specs = (
        P("dp", "seq", None),
        P("dp", "seq", None),
        P(None, "dp", None),
        P(None, "dp", None),
        P(),
        P(),
    )

    return jax.shard_map(on_device, mesh=mesh, in_specs=in_specs, out_specs=out_specs, check_vma=False)
```

profile of v0, /device:TPU:0, one launch (start us, length us, event | category | flops | bytes accessed | tf_op | source)
XLA Modules:
  0.0 157.7 jit_solution(6640309317707104387)
XLA Ops:
  0.6 1.7 %constant_dynamic-slice_fusion = bf16[2,1,128,512]{3,2,1,0:T(8,128)(2,1)} fusion(bf16[2,2,128,512]{3,2,1,0:T(8,128)(2,1)} %bitcast.14, s32[]{:T(128)S(6)} %select_n.4), kind=kLoop, calls=%fused_computation.45 | loop fusion | bytes 524292 | tf_op jit(solution)/shard_map/jit(dynamic_index_in_dim)/dynamic_slice | solution.py:487
  2.3 3.0 %collective-permute-start.1 = (bf16[256,512]{1,0:T(8,128)(2,1)}, bf16[256,512]{1,0:T(8,128)(2,1)S(1)}, u32[]{:S(2)}, u32[]{:S(2)}) collective-permute-start(bf16[256,512]{1,0:T(8,128)(2,1)} %bitcast.4), channel_id=1, source_target_pairs={{0,1},{1,0},{2,3},{3,2},{4,5},{5,4},{6,7},{7,6},{8,9},{9,8},{10,11... | collective-permute-start | bytes 786440 | tf_op jit(solution)/shard_map/ppermute | solution.py:377
  5.3 2.3 %copy-done = bf16[2,512,2176]{2,1,0:T(8,128)(2,1)S(1)} copy-done((bf16[2,512,2176]{2,1,0:T(8,128)(2,1)S(1)}, bf16[2,512,2176]{2,1,0:T(8,128)(2,1)}, u32[]{:S(2)}) %copy-start) | copy-done | bytes 4456472
  7.6 1.0 copy-done.2
  8.6 0.7 copy-done.5
  9.3 1.6 %copy-done.7 = bf16[2,1024,512]{2,1,0:T(8,128)(2,1)S(1)} copy-done((bf16[2,1024,512]{2,1,0:T(8,128)(2,1)S(1)}, bf16[2,1024,512]{2,1,0:T(8,128)(2,1)}, u32[]{:S(2)}) %copy-start.7) | copy-done | bytes 2097176
  10.9 0.7 copy-done.9
  11.6 3.8 %shard_map.109 = (bf16[256,512]{1,0:T(8,128)(2,1)S(1)}, bf16[256,512]{1,0:T(8,128)(2,1)S(1)}, bf16[512,512]{1,0:T(8,128)(2,1)S(1)}, bf16[512,2176]{1,0:T(8,128)(2,1)S(1)}) custom-call(s32[1]{0:T(128)} %bitcast.refs_0_, bf16[2,256,512]{2,1,0:T(8,128)(2,1)S(1)} %bitcast.12, bf16[2,512,2176]{2,1,0:T(8,128)(2,1)S(1)} %copy-done, ...), custom_call_target="tpu_custom_call" | custom-call | flops 2281701376 | bytes 4194304 | tf_op jit(solution)/shard_map/pallas_call | solution.py:363
  15.4 1.4 copy-done.11
  16.8 0.8 copy-done.13
  17.6 0.7 copy-done.15
  18.3 7.8 %collective-permute-done.refs_7_ = bf16[256,512]{1,0:T(8,128)(2,1)S(1)} collective-permute-done((bf16[256,512]{1,0:T(8,128)(2,1)S(1)}, bf16[256,512]{1,0:T(8,128)(2,1)S(1)}, u32[]{:S(2)}, u32[]{:S(2)}) %collective-permute-start) | collective-permute-done | bytes 262176 | tf_op jit(solution)/shard_map/ppermute | solution.py:377
  26.1 2.3 %copy-done.1 = bf16[2,512,2176]{2,1,0:T(8,128)(2,1)S(1)} copy-done((bf16[2,512,2176]{2,1,0:T(8,128)(2,1)S(1)}, bf16[2,512,2176]{2,1,0:T(8,128)(2,1)}, u32[]{:S(2)}) %copy-start.1) | copy-done | bytes 4456472
  28.3 0.9 copy-done.16
  29.3 8.1 %shard_map.110 = (bf16[256,512]{1,0:T(8,128)(2,1)S(1)}, bf16[256,512]{1,0:T(8,128)(2,1)S(1)}, bf16[256,512]{1,0:T(8,128)(2,1)S(1)}, bf16[256,512]{1,0:T(8,128)(2...) custom-call(s32[1]{0:T(128)} %bitcast.refs_0_, ...), custom_call_target="tpu_custom_call" | custom-call | flops 4563402752 | bytes 4194304 | tf_op jit(solution)/shard_map/pallas_call | solution.py:363
  37.4 2.2 %shard_map.114 = (bf16[8,32,3200]{2,1,0:T(8,128)(2,1)S(1)}, bf16[8,32,3200]{2,1,0:T(8,128)(2,1)S(1)}) custom-call(s32[1]{0:T(128)} %bitcast.7.refs_0_, bf16[512,512]{1,0:T(8,128)(2,1)S(1)} %get-tuple-element.74.refs_1_, bf16[512,2176]{1,0:T(8,128)(2,1)S(1)} %get-tuple-element.75.refs_2_, bf16[512,1024]{1,0:T(8,128)(2,1)S(1)} %get-tuple-element.76.refs_3_, ...), custom_call_target="tpu_custom_call" | custom-call | flops 1677721600 | bytes 4194304 | tf_op jit(solution)/shard_map/pallas_call | solution.py:363
  39.8 0.4 collective-permute-start.2
  40.1 8.4 %collective-permute-done.2.refs_3_ = bf16[256,512]{1,0:T(8,128)(2,1)S(1)} collective-permute-done((bf16[256,512]{1,0:T(8,128)(2,1)S(1)}, bf16[256,512]{1,0:T(8,128)(2,1)S(1)}, u32[]{:S(2)}, u32[]{:S(2)}) %collective-permute-start.2) | collective-permute-done | bytes 262176 | tf_op jit(solution)/shard_map/ppermute | solution.py:377
  48.5 4.0 %shard_map.111 = (bf16[512,512]{1,0:T(8,128)(2,1)S(1)}, bf16[512,2176]{1,0:T(8,128)(2,1)S(1)}, bf16[512,1024]{1,0:T(8,128)(2,1)S(1)}, f32[2,128]{1,0:T(2,128)S(1)}) custom-call(bf16[2,1024,512]{2,1,0:T(8,128)(2,1)S(1)} %copy-done.8, f32[2,2,128]{2,1,0:T(2,128)S(1)} %copy-done.10, bf16[256,512]{1,0:T(8,128)(2,1)S(1)} %get-tuple-element.54.refs_2_, ...), custom_call_target="tpu_custom_call" | custom-call | flops 2281701376 | bytes 4194304 | tf_op jit(solution)/shard_map/pallas_call | solution.py:363
  52.5 2.3 %shard_map.113 = (bf16[8,32,1536]{2,1,0:T(8,128)(2,1)S(1)}, bf16[8,32,1536]{2,1,0:T(8,128)(2,1)S(1)}, bf16[8,32,1664]{2,1,0:T(8,128)(2,1)S(1)}, bf16[8,32,1664]{2,1,0:T(8,128)(2,1)S(1)}) custom-call(s32[1]{0:T(128)} %bitcast.7.refs_0_, bf16[512,512]{1,0:T(8,128)(2,1)S(1)} %copy-done.14, bf16[512,2176]{1,0:T(8,128)(2,1)S(1)} %get-tuple-element.60.refs_5_.refs_2_, ...), custom_call_target="tpu_custom_call" | custom-call | flops 1677721600 | bytes 4194304 | tf_op jit(solution)/shard_map/pallas_call | solution.py:363
  54.8 0.2 convert_element_type.143
  55.1 0.6 collective-permute-start.6
  55.6 0.1 convert_element_type.140
  55.8 0.2 convert_element_type.135
  55.9 1.2 collective-permute-done.5
  57.1 0.2 convert_element_type.136
  57.3 0.2 convert_element_type.144
  57.5 0.3 fusion.4
  57.9 3.7 %collective-permute-start.8 = (bf16[4,32,3200]{2,1,0:T(8,128)(2,1)S(1)}, bf16[4,32,3200]{2,1,0:T(8,128)(2,1)S(1)}, u32[]{:S(2)}, u32[]{:S(2)}) collective-permute-start(bf16[4,32,3200]{2,1,0:T(8,128)(2,1)S(1)} %get-tuple-element.99), channel_id=1, source_target_pairs={{0,24},{2,26},{4,28},{6,30},{8,16},{10,18},{12,20},{14,22},{16,8},... | collective-permute-start | bytes 2457608 | tf_op jit(solution)/shard_map/ppermute | solution.py:377
  61.5 0.2 fusion.15
  61.8 0.1 convert_element_type.141
  61.9 0.2 fusion.9
  62.2 18.0 %collective-permute-done.8 = bf16[4,32,3200]{2,1,0:T(8,128)(2,1)S(1)} collective-permute-done((bf16[4,32,3200]{2,1,0:T(8,128)(2,1)S(1)}, bf16[4,32,3200]{2,1,0:T(8,128)(2,1)S(1)}, u32[]{:S(2)}, u32[]{:S(2)}) %collective-permute-start.8) | collective-permute-done | bytes 819232 | tf_op jit(solution)/shard_map/ppermute | solution.py:377
  80.2 0.1 convert_element_type.148
  80.3 0.2 fusion.12
  80.5 1.6 collective-permute-start.9
  82.1 0.5 collective-permute-start.3
  82.6 6.7 %collective-permute-done.3.refs_9_ = bf16[256,512]{1,0:T(8,128)(2,1)S(1)} collective-permute-done((bf16[256,512]{1,0:T(8,128)(2,1)S(1)}, bf16[256,512]{1,0:T(8,128)(2,1)S(1)}, u32[]{:S(2)}, u32[]{:S(2)}) %collective-permute-start.3) | collective-permute-done | bytes 262176 | tf_op jit(solution)/shard_map/ppermute | solution.py:377
  89.3 3.5 %shard_map.112 = (bf16[2,256,512]{2,1,0:T(8,128)(2,1)}, bf16[2,256,512]{2,1,0:T(8,128)(2,1)}, f32[16,128]{1,0:T(8,128)S(1)}) custom-call(s32[1]{0:T(128)} %bitcast.refs_0_, bf16[2,256,512]{2,1,0:T(8,128)(2,1)S(1)} %bitcast.13, bf16[2,512,2176]{2,1,0:T(8,128)(2,1)S(1)} %bitcast.11, f32[2,512]{1,0:T(2,128)S(1)} %copy-done.6, ...), custom_call_target="tpu_custom_call" | custom-call | flops 1140850688 | bytes 4194304 | tf_op jit(solution)/shard_map/pallas_call | solution.py:363
  92.9 1.2 collective-permute-done.4
  94.0 0.5 collective-permute-start.11
  94.6 17.2 %collective-permute-start.10 = (bf16[4,32,1664]{2,1,0:T(8,128)(2,1)S(1)}, bf16[4,32,1664]{2,1,0:T(8,128)(2,1)S(1)}, u32[]{:S(2)}, u32[]{:S(2)}) collective-permute-start(bf16[4,32,1664]{2,1,0:T(8,128)(2,1)S(1)} %get-tuple-element.81), channel_id=1, source_target_pairs={{0,8},{2,10},{4,12},{6,14},{8,0},{10,2},{12,4},{14,6},{16,24},{18,... | collective-permute-start | bytes 1277960 | tf_op jit(solution)/shard_map/ppermute | solution.py:377
  111.8 0.1 fusion.21
  112.0 9.6 %collective-permute-done.10 = bf16[4,32,1664]{2,1,0:T(8,128)(2,1)S(1)} collective-permute-done((bf16[4,32,1664]{2,1,0:T(8,128)(2,1)S(1)}, bf16[4,32,1664]{2,1,0:T(8,128)(2,1)S(1)}, u32[]{:S(2)}, u32[]{:S(2)}) %collective-permute-start.10) | collective-permute-done | bytes 426016 | tf_op jit(solution)/shard_map/ppermute | solution.py:377
  121.7 0.1 fusion.18
  121.8 1.8 %collective-permute-start.13 = (bf16[2,32,1536]{2,1,0:T(8,128)(2,1)S(1)}, bf16[2,32,1536]{2,1,0:T(8,128)(2,1)S(1)}, u32[]{:S(2)}, u32[]{:S(2)}) collective-permute-start(bf16[2,32,1536]{2,1,0:T(8,128)(2,1)S(1)} %get-tuple-element.84), channel_id=1, source_target_pairs={{0,8},{2,10},{4,12},{6,14},{8,0},{10,2},{12,4},{14,6},{16,24},{18,... | collective-permute-start | bytes 589832 | tf_op jit(solution)/shard_map/ppermute | solution.py:377
  123.6 1.5 collective-permute-start.12
  125.1 0.3 collective-permute-start.15
  125.4 2.5 %collective-permute-start.14 = (bf16[2,32,1664]{2,1,0:T(8,128)(2,1)S(1)}, bf16[2,32,1664]{2,1,0:T(8,128)(2,1)S(1)}, u32[]{:S(2)}, u32[]{:S(2)}) collective-permute-start(bf16[2,32,1664]{2,1,0:T(8,128)(2,1)S(1)} %get-tuple-element.85), channel_id=1, source_target_pairs={{0,24},{2,26},{4,28},{6,30},{8,16},{10,18},{12,20},{14,22},{16,8},... | collective-permute-start | bytes 638984 | tf_op jit(solution)/shard_map/ppermute | solution.py:377
  127.8 1.8 %collective-permute-done.13 = bf16[2,32,1536]{2,1,0:T(8,128)(2,1)S(1)} collective-permute-done((bf16[2,32,1536]{2,1,0:T(8,128)(2,1)S(1)}, bf16[2,32,1536]{2,1,0:T(8,128)(2,1)S(1)}, u32[]{:S(2)}, u32[]{:S(2)}) %collective-permute-start.13) | collective-permute-done | bytes 196640 | tf_op jit(solution)/shard_map/ppermute | solution.py:377
  129.7 3.6 %collective-permute-done.15 = bf16[1,32,3200]{2,1,0:T(8,128)(2,1)S(1)} collective-permute-done((bf16[1,32,3200]{2,1,0:T(8,128)(2,1)S(1)}, bf16[1,32,3200]{2,1,0:T(8,128)(2,1)S(1)}, u32[]{:S(2)}, u32[]{:S(2)}) %collective-permute-start.15) | collective-permute-done | bytes 204832 | tf_op jit(solution)/shard_map/ppermute | solution.py:377
  133.3 5.6 %collective-permute-done.14 = bf16[2,32,1664]{2,1,0:T(8,128)(2,1)S(1)} collective-permute-done((bf16[2,32,1664]{2,1,0:T(8,128)(2,1)S(1)}, bf16[2,32,1664]{2,1,0:T(8,128)(2,1)S(1)}, u32[]{:S(2)}, u32[]{:S(2)}) %collective-permute-start.14) | collective-permute-done | bytes 213024 | tf_op jit(solution)/shard_map/ppermute | solution.py:377
  139.0 1.4 collective-permute-start.17
  140.4 1.5 collective-permute-start.18
  141.9 0.5 collective-permute-start.23
  142.4 1.7 %collective-permute-done.16 = f32[16,128]{1,0:T(8,128)S(1)} collective-permute-done((f32[16,128]{1,0:T(8,128)S(1)}, f32[16,128]{1,0:T(8,128)S(1)}, u32[]{:S(2)}, u32[]{:S(2)}) %collective-permute-start.16) | collective-permute-done | bytes 8224 | tf_op jit(solution)/shard_map/ppermute | solution.py:377
  144.1 1.4 collective-permute-done.17
  145.5 0.6 collective-permute-start.22
  146.1 1.5 collective-permute-start.21
  147.6 2.1 %collective-permute-start.19 = (f32[16,128]{1,0:T(8,128)S(1)}, f32[16,128]{1,0:T(8,128)S(1)}, u32[]{:S(2)}, u32[]{:S(2)}) collective-permute-start(f32[16,128]{1,0:T(8,128)S(1)} %add.99), channel_id=1, source_target_pairs={{0,24},{2,26},{4,28},{6,30},{8,16},{10,18},{12,20},{14,22},{16,8},... | collective-permute-start | bytes 24584 | tf_op jit(solution)/shard_map/ppermute | solution.py:377
  149.7 3.4 %collective-permute-done.19 = f32[16,128]{1,0:T(8,128)S(1)} collective-permute-done((f32[16,128]{1,0:T(8,128)S(1)}, f32[16,128]{1,0:T(8,128)S(1)}, u32[]{:S(2)}, u32[]{:S(2)}) %collective-permute-start.19) | collective-permute-done | bytes 8224 | tf_op jit(solution)/shard_map/ppermute | solution.py:377
  153.1 0.5 collective-permute-start.20
  153.6 3.1 %collective-permute-done.20.refs_1_ = f32[16,128]{1,0:T(8,128)S(1)} collective-permute-done((f32[16,128]{1,0:T(8,128)S(1)}, f32[16,128]{1,0:T(8,128)S(1)}, u32[]{:S(2)}, u32[]{:S(2)}) %collective-permute-start.20) | collective-permute-done | bytes 8224 | tf_op jit(solution)/shard_map/ppermute | solution.py:377
  156.7 0.9 shard_map.115
  (59 shorter events, 0.8 us)
Async XLA Ops:
  2.3 16.0 %collective-permute-start.1 = (bf16[256,512]{1,0:T(8,128)(2,1)}, bf16[256,512]{1,0:T(8,128)(2,1)S(1)}, u32[]{:S(2)}, u32[]{:S(2)}) collective-permute-start(bf16[256,512]{1,0:T(8,128)(2,1)} %bitcast.4), channel_id=1, source_target_pairs={{0,1},{1,0},{2,3},{3,2},{4,5},{5,4},{6,7},{7,6},{8,9},{9,8},{10,11... | collective-permute-start | bytes 786440 | tf_op jit(solution)/shard_map/ppermute | solution.py:377
  5.3 2.3 %copy-start = (bf16[2,512,2176]{2,1,0:T(8,128)(2,1)S(1)}, bf16[2,512,2176]{2,1,0:T(8,128)(2,1)}, u32[]{:S(2)}) copy-start(bf16[2,512,2176]{2,1,0:T(8,128)(2,1)} %refs_2_.5) | copy-start | bytes 13369348
  7.6 1.0 copy-start.2
  8.6 0.7 copy-start.5
  9.3 1.6 %copy-start.7 = (bf16[2,1024,512]{2,1,0:T(8,128)(2,1)S(1)}, bf16[2,1024,512]{2,1,0:T(8,128)(2,1)}, u32[]{:S(2)}) copy-start(bf16[2,1024,512]{2,1,0:T(8,128)(2,1)} %refs_0_.1) | copy-start | bytes 6291460
  10.9 0.7 copy-start.9
  11.6 14.5 %copy-start.4 = (bf16[1,512,512]{2,1,0:T(8,128)(2,1)S(1)}, bf16[1,512,512]{2,1,0:T(8,128)(2,1)}, u32[]{:S(2)}) copy-start(bf16[1,512,512]{2,1,0:T(8,128)(2,1)} %param.7) | copy-start | bytes 1572868
  11.6 14.5 %copy-start.6 = (f32[2,512]{1,0:T(2,128)S(1)}, f32[2,512]{1,0:T(2,128)}, u32[]{:S(2)}) copy-start(f32[2,512]{1,0:T(2,128)} %refs_3_.5) | copy-start | bytes 12292
  11.6 14.5 %copy-start.8 = (bf16[2,1024,512]{2,1,0:T(8,128)(2,1)S(1)}, bf16[2,1024,512]{2,1,0:T(8,128)(2,1)}, u32[]{:S(2)}) copy-start(bf16[2,1024,512]{2,1,0:T(8,128)(2,1)} %refs_0_.1) | copy-start | bytes 6291460
  11.6 14.5 %copy-start.10 = (f32[2,2,128]{2,1,0:T(2,128)S(1)}, f32[2,2,128]{2,1,0:T(2,128)}, u32[]{:S(2)}) copy-start(f32[2,2,128]{2,1,0:T(2,128)} %refs_1_.1) | copy-start | bytes 6148
  15.4 1.4 copy-start.11
  16.8 0.8 copy-start.13
  17.6 0.7 copy-start.15
  18.3 7.8 %collective-permute-start = (bf16[256,512]{1,0:T(8,128)(2,1)S(1)}, bf16[256,512]{1,0:T(8,128)(2,1)S(1)}, u32[]{:S(2)}, u32[]{:S(2)}) collective-permute-start(bf16[256,512]{1,0:T(8,128)(2,1)S(1)} %get-tuple-element.53), channel_id=1, source_target_pairs={{0,1},{1,0},{2,3},{3,2},{4,5},{5,4},{6,7},{7,6},{8,9},{9,8},{10,11... | collective-permute-start | bytes 786440 | tf_op jit(solution)/shard_map/ppermute | solution.py:377
  26.1 2.3 %copy-start.1 = (bf16[2,512,2176]{2,1,0:T(8,128)(2,1)S(1)}, bf16[2,512,2176]{2,1,0:T(8,128)(2,1)}, u32[]{:S(2)}) copy-start(bf16[2,512,2176]{2,1,0:T(8,128)(2,1)} %refs_2_.5) | copy-start | bytes 13369348
  28.3 0.9 copy-start.16
  37.4 11.0 %copy-start.12 = (bf16[512,2176]{1,0:T(8,128)(2,1)S(1)}, bf16[512,2176]{1,0:T(8,128)(2,1)}, u32[]{:S(2)}) copy-start(bf16[512,2176]{1,0:T(8,128)(2,1)} %copy-done.11) | copy-start | bytes 6684676
  39.7 17.6 %collective-permute-start.7 = (bf16[8,32,3200]{2,1,0:T(8,128)(2,1)S(1)}, bf16[8,32,3200]{2,1,0:T(8,128)(2,1)S(1)}, u32[]{:S(2)}, u32[]{:S(2)}) collective-permute-start(bf16[8,32,3200]{2,1,0:T(8,128)(2,1)S(1)} %get-tuple-element.79), channel_id=1, source_target_pairs={{0,2},{2,0},{4,6},{6,4},{8,10},{10,8},{12,14},{14,12},{16,18},{18,... | collective-permute-start | bytes 4915208 | tf_op jit(solution)/shard_map/ppermute | solution.py:377
  39.8 8.7 %collective-permute-start.2 = (bf16[256,512]{1,0:T(8,128)(2,1)S(1)}, bf16[256,512]{1,0:T(8,128)(2,1)S(1)}, u32[]{:S(2)}, u32[]{:S(2)}) collective-permute-start(bf16[256,512]{1,0:T(8,128)(2,1)S(1)} %get-tuple-element.56), channel_id=1, source_target_pairs={{0,1},{1,0},{2,3},{3,2},{4,5},{5,4},{6,7},{7,6},{8,9},{9,8},{10,11... | collective-permute-start | bytes 786440 | tf_op jit(solution)/shard_map/ppermute | solution.py:377
  48.5 4.0 %copy-start.14 = (bf16[512,512]{1,0:T(8,128)(2,1)S(1)}, bf16[512,512]{1,0:T(8,128)(2,1)}, u32[]{:S(2)}) copy-start(bf16[512,512]{1,0:T(8,128)(2,1)} %copy-done.13) | copy-start | bytes 1572868
  54.7 2.4 %collective-permute-start.5 = (bf16[8,32,1536]{2,1,0:T(8,128)(2,1)S(1)}, bf16[8,32,1536]{2,1,0:T(8,128)(2,1)S(1)}, u32[]{:S(2)}, u32[]{:S(2)}) collective-permute-start(bf16[8,32,1536]{2,1,0:T(8,128)(2,1)S(1)} %get-tuple-element.71), channel_id=1, source_target_pairs={{0,2},{2,0},{4,6},{6,4},{8,10},{10,8},{12,14},{14,12},{16,18},{18,... | collective-permute-start | bytes 2359304 | tf_op jit(solution)/shard_map/ppermute | solution.py:377
  55.1 6.7 %collective-permute-start.6 = (bf16[8,32,1664]{2,1,0:T(8,128)(2,1)S(1)}, bf16[8,32,1664]{2,1,0:T(8,128)(2,1)S(1)}, u32[]{:S(2)}, u32[]{:S(2)}) collective-permute-start(bf16[8,32,1664]{2,1,0:T(8,128)(2,1)S(1)} %get-tuple-element.73), channel_id=1, source_target_pairs={{0,2},{2,0},{4,6},{6,4},{8,10},{10,8},{12,14},{14,12},{16,18},{18,... | collective-permute-start | bytes 2555912 | tf_op jit(solution)/shard_map/ppermute | solution.py:377
  57.9 22.3 %collective-permute-start.8 = (bf16[4,32,3200]{2,1,0:T(8,128)(2,1)S(1)}, bf16[4,32,3200]{2,1,0:T(8,128)(2,1)S(1)}, u32[]{:S(2)}, u32[]{:S(2)}) collective-permute-start(bf16[4,32,3200]{2,1,0:T(8,128)(2,1)S(1)} %get-tuple-element.99), channel_id=1, source_target_pairs={{0,24},{2,26},{4,28},{6,30},{8,16},{10,18},{12,20},{14,22},{16,8},... | collective-permute-start | bytes 2457608 | tf_op jit(solution)/shard_map/ppermute | solution.py:377
  61.8 27.5 %slice-start = ((s8[4456448]{0:T(1024)(128)(4,1)}), s8[4194304]{0:T(1024)(128)(4,1)S(1)}, s32[]{:S(2)}) async-start(s8[4456448]{0:T(1024)(128)(4,1)} %bitcast.10), calls=%async_computation | async-start | bytes 8388608
  61.9 27.4 %slice-start.1 = ((s8[4456448]{0:T(1024)(128)(4,1)}), s8[262144]{0:T(1024)(128)(4,1)S(1)}, s32[]{:S(2)}) async-start(s8[4456448]{0:T(1024)(128)(4,1)} %bitcast.10), calls=%async_computation.1 | async-start | bytes 524288
  80.3 9.0 %copy-start.3 = (bf16[1,512,512]{2,1,0:T(8,128)(2,1)S(1)}, bf16[1,512,512]{2,1,0:T(8,128)(2,1)}, u32[]{:S(2)}) copy-start(bf16[1,512,512]{2,1,0:T(8,128)(2,1)} %param.6) | copy-start | bytes 1572868
  80.5 31.2 %collective-permute-start.9 = (bf16[4,32,1536]{2,1,0:T(8,128)(2,1)S(1)}, bf16[4,32,1536]{2,1,0:T(8,128)(2,1)S(1)}, u32[]{:S(2)}, u32[]{:S(2)}) collective-permute-start(bf16[4,32,1536]{2,1,0:T(8,128)(2,1)S(1)} %get-tuple-element.80), channel_id=1, source_target_pairs={{0,4},{2,6},{4,0},{6,2},{8,12},{10,14},{12,8},{14,10},{16,20},{18,... | collective-permute-start | bytes 1179656 | tf_op jit(solution)/shard_map/ppermute | solution.py:377
  82.1 7.2 %collective-permute-start.3 = (bf16[256,512]{1,0:T(8,128)(2,1)S(1)}, bf16[256,512]{1,0:T(8,128)(2,1)S(1)}, u32[]{:S(2)}, u32[]{:S(2)}) collective-permute-start(bf16[256,512]{1,0:T(8,128)(2,1)S(1)} %get-tuple-element.64), channel_id=1, source_target_pairs={{0,1},{1,0},{2,3},{3,2},{4,5},{5,4},{6,7},{7,6},{8,9},{9,8},{10,11... | collective-permute-start | bytes 786440 | tf_op jit(solution)/shard_map/ppermute | solution.py:377
  92.8 1.2 collective-permute-start.4
  94.0 17.9 %collective-permute-start.11 = (bf16[2,32,3200]{2,1,0:T(8,128)(2,1)S(1)}, bf16[2,32,3200]{2,1,0:T(8,128)(2,1)S(1)}, u32[]{:S(2)}, u32[]{:S(2)}) collective-permute-start(bf16[2,32,3200]{2,1,0:T(8,128)(2,1)S(1)} %get-tuple-element.82), channel_id=1, source_target_pairs={{0,4},{2,6},{4,0},{6,2},{8,12},{10,14},{12,8},{14,10},{16,20},{18,... | collective-permute-start | bytes 1228808 | tf_op jit(solution)/shard_map/ppermute | solution.py:377
  94.6 27.0 %collective-permute-start.10 = (bf16[4,32,1664]{2,1,0:T(8,128)(2,1)S(1)}, bf16[4,32,1664]{2,1,0:T(8,128)(2,1)S(1)}, u32[]{:S(2)}, u32[]{:S(2)}) collective-permute-start(bf16[4,32,1664]{2,1,0:T(8,128)(2,1)S(1)} %get-tuple-element.81), channel_id=1, source_target_pairs={{0,8},{2,10},{4,12},{6,14},{8,0},{10,2},{12,4},{14,6},{16,24},{18,... | collective-permute-start | bytes 1277960 | tf_op jit(solution)/shard_map/ppermute | solution.py:377
  121.8 7.8 %collective-permute-start.13 = (bf16[2,32,1536]{2,1,0:T(8,128)(2,1)S(1)}, bf16[2,32,1536]{2,1,0:T(8,128)(2,1)S(1)}, u32[]{:S(2)}, u32[]{:S(2)}) collective-permute-start(bf16[2,32,1536]{2,1,0:T(8,128)(2,1)S(1)} %get-tuple-element.84), channel_id=1, source_target_pairs={{0,8},{2,10},{4,12},{6,14},{8,0},{10,2},{12,4},{14,6},{16,24},{18,... | collective-permute-start | bytes 589832 | tf_op jit(solution)/shard_map/ppermute | solution.py:377
  123.6 4.2 %collective-permute-start.12 = (f32[16,128]{1,0:T(8,128)S(1)}, f32[16,128]{1,0:T(8,128)S(1)}, u32[]{:S(2)}, u32[]{:S(2)}) collective-permute-start(f32[16,128]{1,0:T(8,128)S(1)} %add.80), channel_id=1, source_target_pairs={{0,4},{2,6},{4,0},{6,2},{8,12},{10,14},{12,8},{14,10},{16,20},{18,... | collective-permute-start | bytes 24584 | tf_op jit(solution)/shard_map/ppermute | solution.py:377
  125.1 8.2 %collective-permute-start.15 = (bf16[1,32,3200]{2,1,0:T(8,128)(2,1)S(1)}, bf16[1,32,3200]{2,1,0:T(8,128)(2,1)S(1)}, u32[]{:S(2)}, u32[]{:S(2)}) collective-permute-start(bf16[1,32,3200]{2,1,0:T(8,128)(2,1)S(1)} %fusion.14), channel_id=1, source_target_pairs={{0,8},{2,10},{4,12},{6,14},{8,0},{10,2},{12,4},{14,6},{16,24},{18,... | collective-permute-start | bytes 614408 | tf_op jit(solution)/shard_map/ppermute | solution.py:377
  125.4 13.5 %collective-permute-start.14 = (bf16[2,32,1664]{2,1,0:T(8,128)(2,1)S(1)}, bf16[2,32,1664]{2,1,0:T(8,128)(2,1)S(1)}, u32[]{:S(2)}, u32[]{:S(2)}) collective-permute-start(bf16[2,32,1664]{2,1,0:T(8,128)(2,1)S(1)} %get-tuple-element.85), channel_id=1, source_target_pairs={{0,24},{2,26},{4,28},{6,30},{8,16},{10,18},{12,20},{14,22},{16,8},... | collective-permute-start | bytes 638984 | tf_op jit(solution)/shard_map/ppermute | solution.py:377
  139.0 6.5 %collective-permute-start.17 = (bf16[1,32,1536]{2,1,0:T(8,128)(2,1)S(1)}, bf16[1,32,1536]{2,1,0:T(8,128)(2,1)S(1)}, u32[]{:S(2)}, u32[]{:S(2)}) collective-permute-start(bf16[1,32,1536]{2,1,0:T(8,128)(2,1)S(1)} %fusion.23), channel_id=1, source_target_pairs={{0,24},{2,26},{4,28},{6,30},{8,16},{10,18},{12,20},{14,22},{16,8},... | collective-permute-start | bytes 294920 | tf_op jit(solution)/shard_map/ppermute | solution.py:377
  140.4 3.7 %collective-permute-start.16 = (f32[16,128]{1,0:T(8,128)S(1)}, f32[16,128]{1,0:T(8,128)S(1)}, u32[]{:S(2)}, u32[]{:S(2)}) collective-permute-start(f32[16,128]{1,0:T(8,128)S(1)} %add.92), channel_id=1, source_target_pairs={{0,8},{2,10},{4,12},{6,14},{8,0},{10,2},{12,4},{14,6},{16,24},{18,... | collective-permute-start | bytes 24584 | tf_op jit(solution)/shard_map/ppermute | solution.py:377
  140.4 5.1 %collective-permute-start.18 = (bf16[1,32,1664]{2,1,0:T(8,128)(2,1)S(1)}, bf16[1,32,1664]{2,1,0:T(8,128)(2,1)S(1)}, u32[]{:S(2)}, u32[]{:S(2)}) collective-permute-start(bf16[1,32,1664]{2,1,0:T(8,128)(2,1)S(1)} %fusion.20), channel_id=1, source_target_pairs={{0,4},{2,6},{4,0},{6,2},{8,12},{10,14},{12,8},{14,10},{16,20},{18,... | collective-permute-start | bytes 319496 | tf_op jit(solution)/shard_map/ppermute | solution.py:377
  141.9 14.8 %collective-permute-start.23 = (bf16[1,32,3200]{2,1,0:T(8,128)(2,1)S(1)}, bf16[1,32,3200]{2,1,0:T(8,128)(2,1)S(1)}, u32[]{:S(2)}, u32[]{:S(2)}) collective-permute-start(bf16[1,32,3200]{2,1,0:T(8,128)(2,1)S(1)} %add_convert_fusion.refs_6_), channel_id=1, source_target_pairs={{0,1},{1,0},{2,3},{3,2},{4,5},{5,4},{6,7},{7,6},{8,9},{9,8},{10,11... | collective-permute-start | bytes 614408 | tf_op jit(solution)/shard_map/ppermute | solution.py:377
  145.5 11.2 %collective-permute-start.22 = (bf16[1,32,1664]{2,1,0:T(8,128)(2,1)S(1)}, bf16[1,32,1664]{2,1,0:T(8,128)(2,1)S(1)}, u32[]{:S(2)}, u32[]{:S(2)}) collective-permute-start(bf16[1,32,1664]{2,1,0:T(8,128)(2,1)S(1)} %add_convert_fusion.1.refs_4_), channel_id=1, source_target_pairs={{0,1},{1,0},{2,3},{3,2},{4,5},{5,4},{6,7},{7,6},{8,9},{9,8},{10,11... | collective-permute-start | bytes 319496 | tf_op jit(solution)/shard_map/ppermute | solution.py:377
  146.1 10.6 %collective-permute-start.21 = (bf16[1,32,1536]{2,1,0:T(8,128)(2,1)S(1)}, bf16[1,32,1536]{2,1,0:T(8,128)(2,1)S(1)}, u32[]{:S(2)}, u32[]{:S(2)}) collective-permute-start(bf16[1,32,1536]{2,1,0:T(8,128)(2,1)S(1)} %add_convert_fusion.2.refs_2_), channel_id=1, source_target_pairs={{0,1},{1,0},{2,3},{3,2},{4,5},{5,4},{6,7},{7,6},{8,9},{9,8},{10,11... | collective-permute-start | bytes 294920 | tf_op jit(solution)/shard_map/ppermute | solution.py:377
  147.6 5.4 %collective-permute-start.19 = (f32[16,128]{1,0:T(8,128)S(1)}, f32[16,128]{1,0:T(8,128)S(1)}, u32[]{:S(2)}, u32[]{:S(2)}) collective-permute-start(f32[16,128]{1,0:T(8,128)S(1)} %add.99), channel_id=1, source_target_pairs={{0,24},{2,26},{4,28},{6,30},{8,16},{10,18},{12,20},{14,22},{16,8},... | collective-permute-start | bytes 24584 | tf_op jit(solution)/shard_map/ppermute | solution.py:377
  153.1 3.7 %collective-permute-start.20 = (f32[16,128]{1,0:T(8,128)S(1)}, f32[16,128]{1,0:T(8,128)S(1)}, u32[]{:S(2)}, u32[]{:S(2)}) collective-permute-start(f32[16,128]{1,0:T(8,128)S(1)} %add.104.refs_0_), channel_id=1, source_target_pairs={{0,1},{1,0},{2,3},{3,2},{4,5},{5,4},{6,7},{7,6},{8,9},{9,8},{10,11... | collective-permute-start | bytes 24584 | tf_op jit(solution)/shard_map/ppermute | solution.py:377
where the time goes:
time: 158 us
  waiting for transfers between devices  73.2 us (46%)
  starting transfers between devices  41.7 us (26%)
  Pallas kernels  24.8 us (16%)
  local copies, waits for them, and re-layouts  14.1 us (9%)
  other arithmetic  2.89 us (2%)
    ppermute x24, waiting for transfers between devices, swapped(): lax.ppermute(values, axis, [(i, i ^ mask) for i in range(lax.axis_size(ax...  73.2 us
    ppermute x24, starting transfers between devices, swapped(): lax.ppermute(values, axis, [(i, i ^ mask) for i in range(lax.axis_size(ax...  41.7 us
    pallas_call x7, Pallas kernels, run(): pl.pallas_call(kernel, out_shape=[jax.ShapeDtypeStruct(s, d) for s, d in...  24.8 us
    unnamed x38, local copies, waits for them, and re-layouts  12.4 us
  transfers between devices with their start and end apart: 24, of which 14 were waited for; matrix products, arithmetic and copies ran while one was open for 1% of the time, Pallas kernels for 9%

commit v1 on v0

--- a/solution.py
+++ b/solution.py
@@ -322,7 +322,7 @@
 VMEM = pltpu.MemorySpace.VMEM
 SMEM = pltpu.MemorySpace.SMEM
 HBM = pltpu.MemorySpace.HBM
-LIMIT = 28 * 2**20
+LIMITS = {"first": 62, "second": 48, "late": 48, "third": 48, "early": 48, "fourth": 48, "last": 28}
 
 
 class Fetched:
@@ -343,7 +343,7 @@
         return self.now()[index]
 
 
-def run(body, ins, outs, scratch, flops):
+def run(name, body, ins, outs, scratch, flops):
     kinds = [len(v) if isinstance(v, tuple) else 0 for v in ins]
     fetched = [i for i, kind in enumerate(kinds) if kind == 2]
     specs = [pl.BlockSpec(memory_space=(VMEM, SMEM, HBM)[kind]) for kind in kinds]
@@ -368,7 +368,7 @@
         scratch_shapes=[pltpu.VMEM(s, d) for s, d in scratch]
         + targets
         + ([pltpu.SemaphoreType.DMA((len(fetched),))] if fetched else []),
-        compiler_params=pltpu.CompilerParams(vmem_limit_bytes=LIMIT),
+        compiler_params=pltpu.CompilerParams(vmem_limit_bytes=LIMITS[name] * 2**20),
         cost_estimate=pl.CostEstimate(flops=flops, bytes_accessed=2**22, transcendentals=0),
     )(*[v[0] if isinstance(v, tuple) else v for v in ins])
 
@@ -378,17 +378,14 @@
 
 
 def masks_of(size):
-    count = size.bit_length() - 1
-    masks = [1 << b for b in range(count)]
-    if count >= 3:
-        masks[-1] |= masks[-2]
+    return [1 << b for b in range(size.bit_length() - 1)]
+
+
+def rotated(masks, turn):
+    masks = list(masks)
+    if turn and len(masks) > 2:
+        masks[1], masks[2] = masks[2], masks[1]
     return masks
-
-
-def rotated(masks, turn):
-    first, *rest = masks
-    turn %= max(len(rest), 1)
-    return [first] + rest[turn:] + rest[:turn]
 
 
 def offsets_of(masks):
@@ -424,28 +421,27 @@
         self.at += 1
         if self.done():
             return
-        kept = self.kept.astype(jnp.float32)
-        came = self.came.astype(jnp.float32)
         if self.at < self.halvings:
-            half = kept.shape[0] // 2
-            self.away = (kept[half:] + came[half:]).astype(jnp.bfloat16)
-            self.kept = (kept[:half] + came[:half]).astype(jnp.bfloat16)
+            half = self.kept.shape[0] // 2
+            self.away = self.kept[half:] + self.came[half:]
+            self.kept = self.kept[:half] + self.came[:half]
         else:
-            self.away = self.kept = (kept + came).astype(jnp.bfloat16)
+            self.away = self.kept = self.kept + self.came
 
     def done(self):
         return self.at == len(self.steps)
 
 
-LATE = (2,)
+LATE = (0, 1)
 EARLY = (0, 1)
 
 
-def unit_chains(plan, turns, scaling, me, hidden, grad_proj, gated, grad_result):
+def unit_chains(name, plan, turns, scaling, me, hidden, grad_proj, gated, grad_result):
     size = lax.axis_size("dp")
     rows = hidden.shape[1] // size
     outs = [((size // 2, rows, stop - start), jnp.bfloat16) for start, stop, _ in plan for _ in range(2)]
     buffers = run(
+        name,
         partial(weights_kernel, plan, size, scaling),
         [(me,), hidden, grad_proj, gated, grad_result],
         outs,
@@ -489,6 +485,7 @@
         ],
     )
     *first, hidden_first, proj_first = run(
+        "first",
         lambda me, x, wi, wo, sc, ga, *rest: first_kernel(
             shape, me, x, wi, wo, sc, Row(ga, 0), *rest
         ),
@@ -499,6 +496,7 @@
     )
     first_came = exchange(first)
     results = run(
+        "second",
         lambda me, dr, wi, wo, sc, ga, *rest: second_kernel(
             shape, slots * blocks, scaling, me, dr, wi, wo, sc, Row(ga, 1), *rest
         ),
@@ -527,7 +525,9 @@
     back_came = exchange(back)
     columns = inner + half * width // hidden_second.shape[1]
     plans = [plan_of(columns, EARLY), plan_of(columns, LATE)]
-    late = unit_chains(plans[1], LATE, scaling, own, hidden_second, dproj_second, gated_second, dresult_second)
+    late = unit_chains(
+        "late", plans[1], LATE, scaling, own, hidden_second, dproj_second, gated_second, dresult_second
+    )
     for chain in late:
         chain.send()
         chain.land()
@@ -536,14 +536,18 @@
     *second_sends, back_came[0] = tied(*second[1:], back_came[0])
     second_came = exchange([None] + second_sends)
     dresult, dproj_first, gated_first, dscale_early = run(
+        "third",
         lambda wo, sc, *rest: third_kernel(shape, wo, sc, *rest),
         [(weight_out, 0), (qk_scales, 0), back[0]] + back_came + [proj_first],
         [((count, width), bf16), ((count, inner), bf16), ((count, half), bf16), ((2, shared), f32)],
         [((count, half), bf16), ((count, half), bf16)],
         2 * flops,
     )
-    early = unit_chains(plans[0], EARLY, scaling, own, hidden_first, dproj_first, gated_first, dresult)
+    early = unit_chains(
+        "early", plans[0], EARLY, scaling, own, hidden_first, dproj_first, gated_first, dresult
+    )
     grad_frames, output, small = run(
+        "fourth",
         lambda me, x, wi, ga, *rest: fourth_kernel(shape, scaling, me, x, wi, Row(ga, 0), *rest),
         [(me,), (blocked, None), (weight_in, 0), (gains, None), dresult, dproj_first, dscale_early, late_small]
         + [second[0]] + second_came,
@@ -574,6 +578,7 @@
         for chain in live:
             chain.land()
     grad_in, grad_out, grad_gains, grad_scales = run(
+        "last",
         partial(last_kernel, plans),
         [small, small_came] + [v for c in early + late for v in (c.kept, c.came)],
         [

time: 158 us -> 128 us (0.81)
  starting transfers between devices: 41.7 us -> 26.3 us
  local copies, waits for them, and re-layouts: 14.1 us -> 1.95 us
  waiting for transfers between devices: 73.2 us -> 61.1 us
  Pallas kernels: 24.8 us -> 36.7 us
  other arithmetic: 2.89 us -> 0.8 us
    ppermute x24 -> x29, starting transfers between devices: 41.7 us -> 26.3 us  [swapped(): lax.ppermute(values, axis, [(i, i ^ mask) for i in range(lax.axis_size(ax...]
    ppermute x24 -> x29, waiting for transfers between devices: 73.2 us -> 61.1 us  [swapped(): lax.ppermute(values, axis, [(i, i ^ mask) for i in range(lax.axis_size(ax...]
    pallas_call x7, Pallas kernels: 24.8 us -> 36.7 us  [run(): pl.pallas_call(kernel, out_shape=[jax.ShapeDtypeStruct(s, d) for s, d in...]
    unnamed x38 -> x16, local copies, waits for them, and re-layouts: 12.4 us -> 0.98 us
    convert_element_type x24 -> x0, other arithmetic: 2.88 us -> none  [the longest x9 1.74 us: land(): kept = self.kept.astype(jnp.float32)]
  transfers between devices with their start and end apart: 24 -> 29, of which waited for: 14 -> 16; matrix products, arithmetic and copies ran while one was open for 1% -> 1% of each run, Pallas kernels for 9% -> 17%
where the time goes in v1:
time: 128 us
  waiting for transfers between devices  61.1 us (48%)
  Pallas kernels  36.7 us (29%)
  starting transfers between devices  26.3 us (21%)
  local copies, waits for them, and re-layouts  1.95 us (2%)
    ppermute x29, waiting for transfers between devices, swapped(): lax.ppermute(values, axis, [(i, i ^ mask) for i in range(lax.axis_size(ax...  61.1 us
    pallas_call x7, Pallas kernels, run(): pl.pallas_call(kernel, out_shape=[jax.ShapeDtypeStruct(s, d) for s, d in...  36.7 us
    ppermute x29, starting transfers between devices, swapped(): lax.ppermute(values, axis, [(i, i ^ mask) for i in range(lax.axis_size(ax...  26.3 us
  transfers between devices with their start and end apart: 29, of which 16 were waited for; matrix products, arithmetic and copies ran while one was open for 1% of the time, Pallas kernels for 17%

profile of v1, /device:TPU:0, one launch (start us, length us, event | category | flops | bytes accessed | tf_op | source)
XLA Modules:
  0.0 127.8 jit_solution(16029687970071929649)
XLA Ops:
  0.6 1.0 constant_dynamic-slice_fusion
  1.6 3.1 %collective-permute-start.1 = (bf16[256,512]{1,0:T(8,128)(2,1)S(1)}, bf16[256,512]{1,0:T(8,128)(2,1)S(1)}, u32[]{:S(2)}, u32[]{:S(2)}) collective-permute-start(bf16[256,512]{1,0:T(8,128)(2,1)S(1)} %bitcast.14), channel_id=1, source_target_pairs={{0,1},{1,0},{2,3},{3,2},{4,5},{5,4},{6,7},{7,6},{8,9},{9,8},{10,11... | collective-permute-start | bytes 786440 | tf_op jit(solution)/shard_map/ppermute | solution.py:377
  4.7 6.0 %shard_map.109 = (bf16[256,512]{1,0:T(8,128)(2,1)}, bf16[256,512]{1,0:T(8,128)(2,1)}, bf16[512,512]{1,0:T(8,128)(2,1)}, bf16[512,2176]{1,0:T(8,128)(2,1)}) custom-call(s32[1]{0:T(128)} %bitcast.refs_0_, bf16[2,256,512]{2,1,0:T(8,128)(2,1)} %bitcast.10, bf16[2,512,2176]{2,1,0:T(8,128)(2,1)} %refs_2_.5, bf16[2,1024,512]{2,1,0:T(8,128)(2,1)} %refs_0_.1, ...), custom_call_target="tpu_custom_call" | custom-call | flops 2281701376 | bytes 4194304 | tf_op jit(solution)/shard_map/pallas_call | solution.py:363
  10.7 0.1 collective-permute-start
  10.8 0.2 collective-permute-done.1.refs_8_
  11.0 7.8 %collective-permute-done.refs_7_ = bf16[256,512]{1,0:T(8,128)(2,1)S(1)} collective-permute-done((bf16[256,512]{1,0:T(8,128)(2,1)}, bf16[256,512]{1,0:T(8,128)(2,1)S(1)}, u32[]{:S(2)}, u32[]{:S(2)}) %collective-permute-start) | collective-permute-done | bytes 262176 | tf_op jit(solution)/shard_map/ppermute | solution.py:377
  18.8 0.0 copy-start.7
  18.8 0.9 copy-done.7
  19.7 10.3 %shard_map.110 = (bf16[256,512]{1,0:T(8,128)(2,1)S(1)}, bf16[256,512]{1,0:T(8,128)(2,1)S(1)}, bf16[256,512]{1,0:T(8,128)(2,1)S(1)}, bf16[256,512]{1,0:T(8,128)(2...) custom-call(s32[1]{0:T(128)} %bitcast.refs_0_, ...), custom_call_target="tpu_custom_call" | custom-call | flops 4563402752 | bytes 4194304 | tf_op jit(solution)/shard_map/pallas_call | solution.py:363
  30.0 0.0 copy-start.4
  30.0 4.0 %shard_map.114 = (bf16[8,32,1536]{2,1,0:T(8,128)(2,1)S(1)}, bf16[8,32,1536]{2,1,0:T(8,128)(2,1)S(1)}, bf16[8,32,1664]{2,1,0:T(8,128)(2,1)S(1)}, bf16[8,32,1664]{2,1,0:T(8,128)(2,1)S(1)}) custom-call(s32[1]{0:T(128)} %bitcast.7.refs_0_, bf16[512,512]{1,0:T(8,128)(2,1)S(1)} %get-tuple-element.79.refs_1_, bf16[512,2176]{1,0:T(8,128)(2,1)} %get-tuple-element.80.refs_2_, ...), custom_call_target="tpu_custom_call" | custom-call | flops 1677721600 | bytes 4194304 | tf_op jit(solution)/shard_map/pallas_call | solution.py:363
  34.1 0.1 collective-permute-start.7
  34.2 0.4 collective-permute-start.2
  34.6 0.2 collective-permute-start.9
  34.7 8.2 %collective-permute-done.2.refs_3_ = bf16[256,512]{1,0:T(8,128)(2,1)S(1)} collective-permute-done((bf16[256,512]{1,0:T(8,128)(2,1)S(1)}, bf16[256,512]{1,0:T(8,128)(2,1)S(1)}, u32[]{:S(2)}, u32[]{:S(2)}) %collective-permute-start.2) | collective-permute-done | bytes 262176 | tf_op jit(solution)/shard_map/ppermute | solution.py:377
  42.9 7.0 %shard_map.111 = (bf16[512,512]{1,0:T(8,128)(2,1)S(1)}, bf16[512,2176]{1,0:T(8,128)(2,1)}, bf16[512,1024]{1,0:T(8,128)(2,1)S(1)}, f32[2,128]{1,0:T(2,128)S(1)}) custom-call(bf16[2,1024,512]{2,1,0:T(8,128)(2,1)S(1)} %copy-done.4, f32[2,2,128]{2,1,0:T(2,128)S(1)} %copy-done.5, bf16[256,512]{1,0:T(8,128)(2,1)S(1)} %get-tuple-element.59.refs_2_, ...), custom_call_target="tpu_custom_call" | custom-call | flops 2281701376 | bytes 4194304 | tf_op jit(solution)/shard_map/pallas_call | solution.py:363
  49.9 3.8 %shard_map.113 = (bf16[8,32,1536]{2,1,0:T(8,128)(2,1)S(1)}, bf16[8,32,1536]{2,1,0:T(8,128)(2,1)S(1)}, bf16[8,32,1664]{2,1,0:T(8,128)(2,1)S(1)}, bf16[8,32,1664]{2,1,0:T(8,128)(2,1)S(1)}) custom-call(s32[1]{0:T(128)} %bitcast.7.refs_0_, bf16[512,512]{1,0:T(8,128)(2,1)S(1)} %copy-done.6, bf16[512,2176]{1,0:T(8,128)(2,1)} %get-tuple-element.65.refs_5_.refs_2_, ...), custom_call_target="tpu_custom_call" | custom-call | flops 1677721600 | bytes 4194304 | tf_op jit(solution)/shard_map/pallas_call | solution.py:363
  53.8 0.1 collective-permute-start.6
  53.9 0.5 collective-permute-start.5
  54.4 0.3 collective-permute-start.3
  54.7 0.1 slice_add_fusion.5
  54.8 1.7 %collective-permute-start.8 = (bf16[4,32,1536]{2,1,0:T(8,128)(2,1)S(1)}, bf16[4,32,1536]{2,1,0:T(8,128)(2,1)S(1)}, u32[]{:S(2)}, u32[]{:S(2)}) collective-permute-start(bf16[4,32,1536]{2,1,0:T(8,128)(2,1)S(1)} %get-tuple-element.115), channel_id=1, source_target_pairs={{0,4},{2,6},{4,0},{6,2},{8,12},{10,14},{12,8},{14,10},{16,20},{18,... | collective-permute-start | bytes 1179656 | tf_op jit(solution)/shard_map/ppermute | solution.py:377
  56.5 0.0 collective-permute-done.9
  56.5 0.1 slice_add_fusion.2
  56.7 1.6 %collective-permute-start.10 = (bf16[4,32,1664]{2,1,0:T(8,128)(2,1)S(1)}, bf16[4,32,1664]{2,1,0:T(8,128)(2,1)S(1)}, u32[]{:S(2)}, u32[]{:S(2)}) collective-permute-start(bf16[4,32,1664]{2,1,0:T(8,128)(2,1)S(1)} %get-tuple-element.111), channel_id=1, source_target_pairs={{0,8},{2,10},{4,12},{6,14},{8,0},{10,2},{12,4},{14,6},{16,24},{18,... | collective-permute-start | bytes 1277960 | tf_op jit(solution)/shard_map/ppermute | solution.py:377
  58.3 0.1 slice_add_fusion.7
  58.4 0.0 copy-start.1
  58.4 0.1 slice_add_fusion
  58.6 7.1 %collective-permute-done.8 = bf16[4,32,1536]{2,1,0:T(8,128)(2,1)S(1)} collective-permute-done((bf16[4,32,1536]{2,1,0:T(8,128)(2,1)S(1)}, bf16[4,32,1536]{2,1,0:T(8,128)(2,1)S(1)}, u32[]{:S(2)}, u32[]{:S(2)}) %collective-permute-start.8) | collective-permute-done | bytes 393248 | tf_op jit(solution)/shard_map/ppermute | solution.py:377
  65.7 2.2 %collective-permute-done.10 = bf16[4,32,1664]{2,1,0:T(8,128)(2,1)S(1)} collective-permute-done((bf16[4,32,1664]{2,1,0:T(8,128)(2,1)S(1)}, bf16[4,32,1664]{2,1,0:T(8,128)(2,1)S(1)}, u32[]{:S(2)}, u32[]{:S(2)}) %collective-permute-start.10) | collective-permute-done | bytes 426016 | tf_op jit(solution)/shard_map/ppermute | solution.py:377
  68.0 0.1 slice_add_fusion.9
  68.0 1.6 %collective-permute-start.13 = (bf16[2,32,1536]{2,1,0:T(8,128)(2,1)S(1)}, bf16[2,32,1536]{2,1,0:T(8,128)(2,1)S(1)}, u32[]{:S(2)}, u32[]{:S(2)}) collective-permute-start(bf16[2,32,1536]{2,1,0:T(8,128)(2,1)S(1)} %get-tuple-element.89), channel_id=1, source_target_pairs={{0,8},{2,10},{4,12},{6,14},{8,0},{10,2},{12,4},{14,6},{16,24},{18,... | collective-permute-start | bytes 589832 | tf_op jit(solution)/shard_map/ppermute | solution.py:377
  69.7 4.5 %shard_map.112 = (bf16[2,256,512]{2,1,0:T(8,128)(2,1)}, bf16[2,256,512]{2,1,0:T(8,128)(2,1)}, f32[16,128]{1,0:T(8,128)S(1)}) custom-call(s32[1]{0:T(128)} %bitcast.refs_0_, bf16[2,256,512]{2,1,0:T(8,128)(2,1)S(1)} %bitcast.11, bf16[2,512,2176]{2,1,0:T(8,128)(2,1)} %refs_2_.5, f32[2,512]{1,0:T(2,128)S(1)} %copy-done.3, ...), custom_call_target="tpu_custom_call" | custom-call | flops 1140850688 | bytes 4194304 | tf_op jit(solution)/shard_map/pallas_call | solution.py:363
  74.2 0.1 collective-permute-start.4
  74.3 1.2 collective-permute-done.4
  75.5 0.5 collective-permute-start.14
  76.0 0.3 collective-permute-start.12
  76.3 1.6 %collective-permute-start.11 = (bf16[4,32,1536]{2,1,0:T(8,128)(2,1)S(1)}, bf16[4,32,1536]{2,1,0:T(8,128)(2,1)S(1)}, u32[]{:S(2)}, u32[]{:S(2)}) collective-permute-start(bf16[4,32,1536]{2,1,0:T(8,128)(2,1)S(1)} %get-tuple-element.87), channel_id=1, source_target_pairs={{0,4},{2,6},{4,0},{6,2},{8,12},{10,14},{12,8},{14,10},{16,20},{18,... | collective-permute-start | bytes 1179656 | tf_op jit(solution)/shard_map/ppermute | solution.py:377
  78.0 5.6 %collective-permute-done.14 = bf16[2,32,1664]{2,1,0:T(8,128)(2,1)S(1)} collective-permute-done((bf16[2,32,1664]{2,1,0:T(8,128)(2,1)S(1)}, bf16[2,32,1664]{2,1,0:T(8,128)(2,1)S(1)}, u32[]{:S(2)}, u32[]{:S(2)}) %collective-permute-start.14) | collective-permute-done | bytes 213024 | tf_op jit(solution)/shard_map/ppermute | solution.py:377
  83.6 7.6 %collective-permute-done.11 = bf16[4,32,1536]{2,1,0:T(8,128)(2,1)S(1)} collective-permute-done((bf16[4,32,1536]{2,1,0:T(8,128)(2,1)S(1)}, bf16[4,32,1536]{2,1,0:T(8,128)(2,1)S(1)}, u32[]{:S(2)}, u32[]{:S(2)}) %collective-permute-start.11) | collective-permute-done | bytes 393248 | tf_op jit(solution)/shard_map/ppermute | solution.py:377
  91.2 0.1 slice_add_fusion.12
  91.3 0.1 slice_add_fusion.8
  91.4 2.7 %collective-permute-start.18 = (bf16[1,32,1536]{2,1,0:T(8,128)(2,1)S(1)}, bf16[1,32,1536]{2,1,0:T(8,128)(2,1)S(1)}, u32[]{:S(2)}, u32[]{:S(2)}) collective-permute-start(bf16[1,32,1536]{2,1,0:T(8,128)(2,1)S(1)} %slice_add_fusion.23), channel_id=1, source_target_pairs={{0,16},{2,18},{4,20},{6,22},{8,24},{10,26},{12,28},{14,30},{16,0},... | collective-permute-start | bytes 294920 | tf_op jit(solution)/shard_map/ppermute | solution.py:377
  94.0 0.5 collective-permute-start.15
  94.5 0.3 collective-permute-start.19
  94.9 1.5 %collective-permute-start.17 = (bf16[2,32,1664]{2,1,0:T(8,128)(2,1)S(1)}, bf16[2,32,1664]{2,1,0:T(8,128)(2,1)S(1)}, u32[]{:S(2)}, u32[]{:S(2)}) collective-permute-start(bf16[2,32,1664]{2,1,0:T(8,128)(2,1)S(1)} %get-tuple-element.93), channel_id=1, source_target_pairs={{0,4},{2,6},{4,0},{6,2},{8,12},{10,14},{12,8},{14,10},{16,20},{18,... | collective-permute-start | bytes 638984 | tf_op jit(solution)/shard_map/ppermute | solution.py:377
  96.4 0.4 collective-permute-start.16
  96.8 0.9 collective-permute-done.15
  97.8 3.5 %collective-permute-done.18 = bf16[1,32,1536]{2,1,0:T(8,128)(2,1)S(1)} collective-permute-done((bf16[1,32,1536]{2,1,0:T(8,128)(2,1)S(1)}, bf16[1,32,1536]{2,1,0:T(8,128)(2,1)S(1)}, u32[]{:S(2)}, u32[]{:S(2)}) %collective-permute-start.18) | collective-permute-done | bytes 98336 | tf_op jit(solution)/shard_map/ppermute | solution.py:377
  101.3 1.6 %collective-permute-done.19 = bf16[1,32,1664]{2,1,0:T(8,128)(2,1)S(1)} collective-permute-done((bf16[1,32,1664]{2,1,0:T(8,128)(2,1)S(1)}, bf16[1,32,1664]{2,1,0:T(8,128)(2,1)S(1)}, u32[]{:S(2)}, u32[]{:S(2)}) %collective-permute-start.19) | collective-permute-done | bytes 106528 | tf_op jit(solution)/shard_map/ppermute | solution.py:377
  102.9 2.2 %collective-permute-done.16 = bf16[2,32,1536]{2,1,0:T(8,128)(2,1)S(1)} collective-permute-done((bf16[2,32,1536]{2,1,0:T(8,128)(2,1)S(1)}, bf16[2,32,1536]{2,1,0:T(8,128)(2,1)S(1)}, u32[]{:S(2)}, u32[]{:S(2)}) %collective-permute-start.16) | collective-permute-done | bytes 196640 | tf_op jit(solution)/shard_map/ppermute | solution.py:377
  105.1 0.2 collective-permute-start.21
  105.3 2.5 %collective-permute-start.20 = (f32[16,128]{1,0:T(8,128)S(1)}, f32[16,128]{1,0:T(8,128)S(1)}, u32[]{:S(2)}, u32[]{:S(2)}) collective-permute-start(f32[16,128]{1,0:T(8,128)S(1)} %add.118), channel_id=1, source_target_pairs={{0,8},{2,10},{4,12},{6,14},{8,0},{10,2},{12,4},{14,6},{16,24},{18,... | collective-permute-start | bytes 24584 | tf_op jit(solution)/shard_map/ppermute | solution.py:377
  107.8 0.3 collective-permute-start.22
  108.1 1.5 %collective-permute-start.28 = (bf16[1,32,1664]{2,1,0:T(8,128)(2,1)S(1)}, bf16[1,32,1664]{2,1,0:T(8,128)(2,1)S(1)}, u32[]{:S(2)}, u32[]{:S(2)}) collective-permute-start(bf16[1,32,1664]{2,1,0:T(8,128)(2,1)S(1)} %fusion.1.refs_8_), channel_id=1, source_target_pairs={{0,1},{1,0},{2,3},{3,2},{4,5},{5,4},{6,7},{7,6},{8,9},{9,8},{10,11... | collective-permute-start | bytes 319496 | tf_op jit(solution)/shard_map/ppermute | solution.py:377
  109.6 4.2 %collective-permute-done.21 = bf16[1,32,1536]{2,1,0:T(8,128)(2,1)S(1)} collective-permute-done((bf16[1,32,1536]{2,1,0:T(8,128)(2,1)S(1)}, bf16[1,32,1536]{2,1,0:T(8,128)(2,1)S(1)}, u32[]{:S(2)}, u32[]{:S(2)}) %collective-permute-start.21) | collective-permute-done | bytes 98336 | tf_op jit(solution)/shard_map/ppermute | solution.py:377
  113.9 1.1 collective-permute-done.22
  115.0 1.6 %collective-permute-start.26 = (bf16[1,32,1664]{2,1,0:T(8,128)(2,1)S(1)}, bf16[1,32,1664]{2,1,0:T(8,128)(2,1)S(1)}, u32[]{:S(2)}, u32[]{:S(2)}) collective-permute-start(bf16[1,32,1664]{2,1,0:T(8,128)(2,1)S(1)} %fusion.refs_4_), channel_id=1, source_target_pairs={{0,1},{1,0},{2,3},{3,2},{4,5},{5,4},{6,7},{7,6},{8,9},{9,8},{10,11... | collective-permute-start | bytes 319496 | tf_op jit(solution)/shard_map/ppermute | solution.py:377
  116.6 0.5 collective-permute-start.27
  117.1 1.5 %collective-permute-start.25 = (bf16[1,32,1536]{2,1,0:T(8,128)(2,1)S(1)}, bf16[1,32,1536]{2,1,0:T(8,128)(2,1)S(1)}, u32[]{:S(2)}, u32[]{:S(2)}) collective-permute-start(bf16[1,32,1536]{2,1,0:T(8,128)(2,1)S(1)} %fusion.2.refs_2_), channel_id=1, source_target_pairs={{0,1},{1,0},{2,3},{3,2},{4,5},{5,4},{6,7},{7,6},{8,9},{9,8},{10,11... | collective-permute-start | bytes 294920 | tf_op jit(solution)/shard_map/ppermute | solution.py:377
  118.6 4.5 %collective-permute-done.23 = f32[16,128]{1,0:T(8,128)S(1)} collective-permute-done((f32[16,128]{1,0:T(8,128)S(1)}, f32[16,128]{1,0:T(8,128)S(1)}, u32[]{:S(2)}, u32[]{:S(2)}) %collective-permute-start.23) | collective-permute-done | bytes 8224 | tf_op jit(solution)/shard_map/ppermute | solution.py:377
  123.2 0.5 collective-permute-start.24
  123.7 3.1 %collective-permute-done.24.refs_1_ = f32[16,128]{1,0:T(8,128)S(1)} collective-permute-done((f32[16,128]{1,0:T(8,128)S(1)}, f32[16,128]{1,0:T(8,128)S(1)}, u32[]{:S(2)}, u32[]{:S(2)}) %collective-permute-start.24) | collective-permute-done | bytes 8224 | tf_op jit(solution)/shard_map/ppermute | solution.py:377
  126.8 0.9 shard_map.115
  (38 shorter events, 0.3 us)
Async XLA Ops:
  1.6 9.4 %collective-permute-start.1 = (bf16[256,512]{1,0:T(8,128)(2,1)S(1)}, bf16[256,512]{1,0:T(8,128)(2,1)S(1)}, u32[]{:S(2)}, u32[]{:S(2)}) collective-permute-start(bf16[256,512]{1,0:T(8,128)(2,1)S(1)} %bitcast.14), channel_id=1, source_target_pairs={{0,1},{1,0},{2,3},{3,2},{4,5},{5,4},{6,7},{7,6},{8,9},{9,8},{10,11... | collective-permute-start | bytes 786440 | tf_op jit(solution)/shard_map/ppermute | solution.py:377
  4.7 14.1 %copy-start.2 = (bf16[1,512,512]{2,1,0:T(8,128)(2,1)S(1)}, bf16[1,512,512]{2,1,0:T(8,128)(2,1)}, u32[]{:S(2)}) copy-start(bf16[1,512,512]{2,1,0:T(8,128)(2,1)} %param.7) | copy-start | bytes 1572868
  4.7 14.1 %copy-start.3 = (f32[2,512]{1,0:T(2,128)S(1)}, f32[2,512]{1,0:T(2,128)}, u32[]{:S(2)}) copy-start(f32[2,512]{1,0:T(2,128)} %refs_3_.5) | copy-start | bytes 12292
  4.7 14.1 %copy-start.5 = (f32[2,2,128]{2,1,0:T(2,128)S(1)}, f32[2,2,128]{2,1,0:T(2,128)}, u32[]{:S(2)}) copy-start(f32[2,2,128]{2,1,0:T(2,128)} %refs_1_.1) | copy-start | bytes 6148
  10.7 8.1 %collective-permute-start = (bf16[256,512]{1,0:T(8,128)(2,1)}, bf16[256,512]{1,0:T(8,128)(2,1)S(1)}, u32[]{:S(2)}, u32[]{:S(2)}) collective-permute-start(bf16[256,512]{1,0:T(8,128)(2,1)} %get-tuple-element.58), channel_id=1, source_target_pairs={{0,1},{1,0},{2,3},{3,2},{4,5},{5,4},{6,7},{7,6},{8,9},{9,8},{10,11... | collective-permute-start | bytes 786440 | tf_op jit(solution)/shard_map/ppermute | solution.py:377
  18.8 1.0 copy-start.7
  30.0 12.9 %copy-start.4 = (bf16[2,1024,512]{2,1,0:T(8,128)(2,1)S(1)}, bf16[2,1024,512]{2,1,0:T(8,128)(2,1)}, u32[]{:S(2)}) copy-start(bf16[2,1024,512]{2,1,0:T(8,128)(2,1)} %refs_0_.1) | copy-start | bytes 6291460
  34.1 20.6 %collective-permute-start.7 = (bf16[8,32,1536]{2,1,0:T(8,128)(2,1)S(1)}, bf16[8,32,1536]{2,1,0:T(8,128)(2,1)S(1)}, u32[]{:S(2)}, u32[]{:S(2)}) collective-permute-start(bf16[8,32,1536]{2,1,0:T(8,128)(2,1)S(1)} %get-tuple-element.84), channel_id=1, source_target_pairs={{0,2},{2,0},{4,6},{6,4},{8,10},{10,8},{12,14},{14,12},{16,18},{18,... | collective-permute-start | bytes 2359304 | tf_op jit(solution)/shard_map/ppermute | solution.py:377
  34.2 8.7 %collective-permute-start.2 = (bf16[256,512]{1,0:T(8,128)(2,1)S(1)}, bf16[256,512]{1,0:T(8,128)(2,1)S(1)}, u32[]{:S(2)}, u32[]{:S(2)}) collective-permute-start(bf16[256,512]{1,0:T(8,128)(2,1)S(1)} %get-tuple-element.61), channel_id=1, source_target_pairs={{0,1},{1,0},{2,3},{3,2},{4,5},{5,4},{6,7},{7,6},{8,9},{9,8},{10,11... | collective-permute-start | bytes 786440 | tf_op jit(solution)/shard_map/ppermute | solution.py:377
  34.6 22.0 %collective-permute-start.9 = (bf16[8,32,1664]{2,1,0:T(8,128)(2,1)S(1)}, bf16[8,32,1664]{2,1,0:T(8,128)(2,1)S(1)}, u32[]{:S(2)}, u32[]{:S(2)}) collective-permute-start(bf16[8,32,1664]{2,1,0:T(8,128)(2,1)S(1)} %get-tuple-element.86), channel_id=1, source_target_pairs={{0,2},{2,0},{4,6},{6,4},{8,10},{10,8},{12,14},{14,12},{16,18},{18,... | collective-permute-start | bytes 2555912 | tf_op jit(solution)/shard_map/ppermute | solution.py:377
  42.9 7.1 %copy-start.6 = (bf16[512,512]{1,0:T(8,128)(2,1)S(1)}, bf16[512,512]{1,0:T(8,128)(2,1)}, u32[]{:S(2)}) copy-start(bf16[512,512]{1,0:T(8,128)(2,1)} %get-tuple-element.73.refs_1_) | copy-start | bytes 1572868
  53.8 4.6 %collective-permute-start.6 = (bf16[8,32,1664]{2,1,0:T(8,128)(2,1)S(1)}, bf16[8,32,1664]{2,1,0:T(8,128)(2,1)S(1)}, u32[]{:S(2)}, u32[]{:S(2)}) collective-permute-start(bf16[8,32,1664]{2,1,0:T(8,128)(2,1)S(1)} %get-tuple-element.78), channel_id=1, source_target_pairs={{0,2},{2,0},{4,6},{6,4},{8,10},{10,8},{12,14},{14,12},{16,18},{18,... | collective-permute-start | bytes 2555912 | tf_op jit(solution)/shard_map/ppermute | solution.py:377
  53.9 4.4 %collective-permute-start.5 = (bf16[8,32,1536]{2,1,0:T(8,128)(2,1)S(1)}, bf16[8,32,1536]{2,1,0:T(8,128)(2,1)S(1)}, u32[]{:S(2)}, u32[]{:S(2)}) collective-permute-start(bf16[8,32,1536]{2,1,0:T(8,128)(2,1)S(1)} %get-tuple-element.76), channel_id=1, source_target_pairs={{0,2},{2,0},{4,6},{6,4},{8,10},{10,8},{12,14},{14,12},{16,18},{18,... | collective-permute-start | bytes 2359304 | tf_op jit(solution)/shard_map/ppermute | solution.py:377
  54.4 15.3 %collective-permute-start.3 = (bf16[256,512]{1,0:T(8,128)(2,1)S(1)}, bf16[256,512]{1,0:T(8,128)(2,1)S(1)}, u32[]{:S(2)}, u32[]{:S(2)}) collective-permute-start(bf16[256,512]{1,0:T(8,128)(2,1)S(1)} %get-tuple-element.69), channel_id=1, source_target_pairs={{0,1},{1,0},{2,3},{3,2},{4,5},{5,4},{6,7},{7,6},{8,9},{9,8},{10,11... | collective-permute-start | bytes 786440 | tf_op jit(solution)/shard_map/ppermute | solution.py:377
  54.8 10.9 %collective-permute-start.8 = (bf16[4,32,1536]{2,1,0:T(8,128)(2,1)S(1)}, bf16[4,32,1536]{2,1,0:T(8,128)(2,1)S(1)}, u32[]{:S(2)}, u32[]{:S(2)}) collective-permute-start(bf16[4,32,1536]{2,1,0:T(8,128)(2,1)S(1)} %get-tuple-element.115), channel_id=1, source_target_pairs={{0,4},{2,6},{4,0},{6,2},{8,12},{10,14},{12,8},{14,10},{16,20},{18,... | collective-permute-start | bytes 1179656 | tf_op jit(solution)/shard_map/ppermute | solution.py:377
  56.7 11.3 %collective-permute-start.10 = (bf16[4,32,1664]{2,1,0:T(8,128)(2,1)S(1)}, bf16[4,32,1664]{2,1,0:T(8,128)(2,1)S(1)}, u32[]{:S(2)}, u32[]{:S(2)}) collective-permute-start(bf16[4,32,1664]{2,1,0:T(8,128)(2,1)S(1)} %get-tuple-element.111), channel_id=1, source_target_pairs={{0,8},{2,10},{4,12},{6,14},{8,0},{10,2},{12,4},{14,6},{16,24},{18,... | collective-permute-start | bytes 1277960 | tf_op jit(solution)/shard_map/ppermute | solution.py:377
  58.4 11.3 %copy-start = (bf16[512,2176]{1,0:T(8,128)(2,1)S(1)}, bf16[512,2176]{1,0:T(8,128)(2,1)}, u32[]{:S(2)}) copy-start(bf16[512,2176]{1,0:T(8,128)(2,1)} %get-tuple-element.65.refs_5_.refs_2_) | copy-start | bytes 6684676
  58.4 11.2 %copy-start.1 = (bf16[1,512,512]{2,1,0:T(8,128)(2,1)S(1)}, bf16[1,512,512]{2,1,0:T(8,128)(2,1)}, u32[]{:S(2)}) copy-start(bf16[1,512,512]{2,1,0:T(8,128)(2,1)} %param.6) | copy-start | bytes 1572868
  68.0 9.9 %collective-permute-start.13 = (bf16[2,32,1536]{2,1,0:T(8,128)(2,1)S(1)}, bf16[2,32,1536]{2,1,0:T(8,128)(2,1)S(1)}, u32[]{:S(2)}, u32[]{:S(2)}) collective-permute-start(bf16[2,32,1536]{2,1,0:T(8,128)(2,1)S(1)} %get-tuple-element.89), channel_id=1, source_target_pairs={{0,8},{2,10},{4,12},{6,14},{8,0},{10,2},{12,4},{14,6},{16,24},{18,... | collective-permute-start | bytes 589832 | tf_op jit(solution)/shard_map/ppermute | solution.py:377
  74.2 1.2 collective-permute-start.4
  75.5 8.1 %collective-permute-start.14 = (bf16[2,32,1664]{2,1,0:T(8,128)(2,1)S(1)}, bf16[2,32,1664]{2,1,0:T(8,128)(2,1)S(1)}, u32[]{:S(2)}, u32[]{:S(2)}) collective-permute-start(bf16[2,32,1664]{2,1,0:T(8,128)(2,1)S(1)} %get-tuple-element.90), channel_id=1, source_target_pairs={{0,4},{2,6},{4,0},{6,2},{8,12},{10,14},{12,8},{14,10},{16,20},{18,... | collective-permute-start | bytes 638984 | tf_op jit(solution)/shard_map/ppermute | solution.py:377
  76.0 15.3 %collective-permute-start.12 = (bf16[4,32,1664]{2,1,0:T(8,128)(2,1)S(1)}, bf16[4,32,1664]{2,1,0:T(8,128)(2,1)S(1)}, u32[]{:S(2)}, u32[]{:S(2)}) collective-permute-start(bf16[4,32,1664]{2,1,0:T(8,128)(2,1)S(1)} %get-tuple-element.88), channel_id=1, source_target_pairs={{0,8},{2,10},{4,12},{6,14},{8,0},{10,2},{12,4},{14,6},{16,24},{18,... | collective-permute-start | bytes 1277960 | tf_op jit(solution)/shard_map/ppermute | solution.py:377
  76.3 14.9 %collective-permute-start.11 = (bf16[4,32,1536]{2,1,0:T(8,128)(2,1)S(1)}, bf16[4,32,1536]{2,1,0:T(8,128)(2,1)S(1)}, u32[]{:S(2)}, u32[]{:S(2)}) collective-permute-start(bf16[4,32,1536]{2,1,0:T(8,128)(2,1)S(1)} %get-tuple-element.87), channel_id=1, source_target_pairs={{0,4},{2,6},{4,0},{6,2},{8,12},{10,14},{12,8},{14,10},{16,20},{18,... | collective-permute-start | bytes 1179656 | tf_op jit(solution)/shard_map/ppermute | solution.py:377
  91.4 10.0 %collective-permute-start.18 = (bf16[1,32,1536]{2,1,0:T(8,128)(2,1)S(1)}, bf16[1,32,1536]{2,1,0:T(8,128)(2,1)S(1)}, u32[]{:S(2)}, u32[]{:S(2)}) collective-permute-start(bf16[1,32,1536]{2,1,0:T(8,128)(2,1)S(1)} %slice_add_fusion.23), channel_id=1, source_target_pairs={{0,16},{2,18},{4,20},{6,22},{8,24},{10,26},{12,28},{14,30},{16,0},... | collective-permute-start | bytes 294920 | tf_op jit(solution)/shard_map/ppermute | solution.py:377
  94.0 3.7 %collective-permute-start.15 = (f32[16,128]{1,0:T(8,128)S(1)}, f32[16,128]{1,0:T(8,128)S(1)}, u32[]{:S(2)}, u32[]{:S(2)}) collective-permute-start(f32[16,128]{1,0:T(8,128)S(1)} %add.101), channel_id=1, source_target_pairs={{0,4},{2,6},{4,0},{6,2},{8,12},{10,14},{12,8},{14,10},{16,20},{18,... | collective-permute-start | bytes 24584 | tf_op jit(solution)/shard_map/ppermute | solution.py:377
  94.5 8.3 %collective-permute-start.19 = (bf16[1,32,1664]{2,1,0:T(8,128)(2,1)S(1)}, bf16[1,32,1664]{2,1,0:T(8,128)(2,1)S(1)}, u32[]{:S(2)}, u32[]{:S(2)}) collective-permute-start(bf16[1,32,1664]{2,1,0:T(8,128)(2,1)S(1)} %slice_add_fusion.19), channel_id=1, source_target_pairs={{0,16},{2,18},{4,20},{6,22},{8,24},{10,26},{12,28},{14,30},{16,0},... | collective-permute-start | bytes 319496 | tf_op jit(solution)/shard_map/ppermute | solution.py:377
  94.9 10.2 %collective-permute-start.17 = (bf16[2,32,1664]{2,1,0:T(8,128)(2,1)S(1)}, bf16[2,32,1664]{2,1,0:T(8,128)(2,1)S(1)}, u32[]{:S(2)}, u32[]{:S(2)}) collective-permute-start(bf16[2,32,1664]{2,1,0:T(8,128)(2,1)S(1)} %get-tuple-element.93), channel_id=1, source_target_pairs={{0,4},{2,6},{4,0},{6,2},{8,12},{10,14},{12,8},{14,10},{16,20},{18,... | collective-permute-start | bytes 638984 | tf_op jit(solution)/shard_map/ppermute | solution.py:377
  96.4 8.7 %collective-permute-start.16 = (bf16[2,32,1536]{2,1,0:T(8,128)(2,1)S(1)}, bf16[2,32,1536]{2,1,0:T(8,128)(2,1)S(1)}, u32[]{:S(2)}, u32[]{:S(2)}) collective-permute-start(bf16[2,32,1536]{2,1,0:T(8,128)(2,1)S(1)} %get-tuple-element.92), channel_id=1, source_target_pairs={{0,8},{2,10},{4,12},{6,14},{8,0},{10,2},{12,4},{14,6},{16,24},{18,... | collective-permute-start | bytes 589832 | tf_op jit(solution)/shard_map/ppermute | solution.py:377
  105.1 8.7 %collective-permute-start.21 = (bf16[1,32,1536]{2,1,0:T(8,128)(2,1)S(1)}, bf16[1,32,1536]{2,1,0:T(8,128)(2,1)S(1)}, u32[]{:S(2)}, u32[]{:S(2)}) collective-permute-start(bf16[1,32,1536]{2,1,0:T(8,128)(2,1)S(1)} %slice_add_fusion.22), channel_id=1, source_target_pairs={{0,16},{2,18},{4,20},{6,22},{8,24},{10,26},{12,28},{14,30},{16,0},... | collective-permute-start | bytes 294920 | tf_op jit(solution)/shard_map/ppermute | solution.py:377
  105.3 4.3 %collective-permute-start.20 = (f32[16,128]{1,0:T(8,128)S(1)}, f32[16,128]{1,0:T(8,128)S(1)}, u32[]{:S(2)}, u32[]{:S(2)}) collective-permute-start(f32[16,128]{1,0:T(8,128)S(1)} %add.118), channel_id=1, source_target_pairs={{0,8},{2,10},{4,12},{6,14},{8,0},{10,2},{12,4},{14,6},{16,24},{18,... | collective-permute-start | bytes 24584 | tf_op jit(solution)/shard_map/ppermute | solution.py:377
  107.8 7.2 %collective-permute-start.22 = (bf16[1,32,1664]{2,1,0:T(8,128)(2,1)S(1)}, bf16[1,32,1664]{2,1,0:T(8,128)(2,1)S(1)}, u32[]{:S(2)}, u32[]{:S(2)}) collective-permute-start(bf16[1,32,1664]{2,1,0:T(8,128)(2,1)S(1)} %slice_add_fusion.18), channel_id=1, source_target_pairs={{0,16},{2,18},{4,20},{6,22},{8,24},{10,26},{12,28},{14,30},{16,0},... | collective-permute-start | bytes 319496 | tf_op jit(solution)/shard_map/ppermute | solution.py:377
  108.1 15.6 %collective-permute-start.28 = (bf16[1,32,1664]{2,1,0:T(8,128)(2,1)S(1)}, bf16[1,32,1664]{2,1,0:T(8,128)(2,1)S(1)}, u32[]{:S(2)}, u32[]{:S(2)}) collective-permute-start(bf16[1,32,1664]{2,1,0:T(8,128)(2,1)S(1)} %fusion.1.refs_8_), channel_id=1, source_target_pairs={{0,1},{1,0},{2,3},{3,2},{4,5},{5,4},{6,7},{7,6},{8,9},{9,8},{10,11... | collective-permute-start | bytes 319496 | tf_op jit(solution)/shard_map/ppermute | solution.py:377
  115.0 11.8 %collective-permute-start.26 = (bf16[1,32,1664]{2,1,0:T(8,128)(2,1)S(1)}, bf16[1,32,1664]{2,1,0:T(8,128)(2,1)S(1)}, u32[]{:S(2)}, u32[]{:S(2)}) collective-permute-start(bf16[1,32,1664]{2,1,0:T(8,128)(2,1)S(1)} %fusion.refs_4_), channel_id=1, source_target_pairs={{0,1},{1,0},{2,3},{3,2},{4,5},{5,4},{6,7},{7,6},{8,9},{9,8},{10,11... | collective-permute-start | bytes 319496 | tf_op jit(solution)/shard_map/ppermute | solution.py:377
  116.6 7.1 %collective-permute-start.27 = (bf16[1,32,1536]{2,1,0:T(8,128)(2,1)S(1)}, bf16[1,32,1536]{2,1,0:T(8,128)(2,1)S(1)}, u32[]{:S(2)}, u32[]{:S(2)}) collective-permute-start(bf16[1,32,1536]{2,1,0:T(8,128)(2,1)S(1)} %fusion.3.refs_6_), channel_id=1, source_target_pairs={{0,1},{1,0},{2,3},{3,2},{4,5},{5,4},{6,7},{7,6},{8,9},{9,8},{10,11... | collective-permute-start | bytes 294920 | tf_op jit(solution)/shard_map/ppermute | solution.py:377
  117.1 9.7 %collective-permute-start.25 = (bf16[1,32,1536]{2,1,0:T(8,128)(2,1)S(1)}, bf16[1,32,1536]{2,1,0:T(8,128)(2,1)S(1)}, u32[]{:S(2)}, u32[]{:S(2)}) collective-permute-start(bf16[1,32,1536]{2,1,0:T(8,128)(2,1)S(1)} %fusion.2.refs_2_), channel_id=1, source_target_pairs={{0,1},{1,0},{2,3},{3,2},{4,5},{5,4},{6,7},{7,6},{8,9},{9,8},{10,11... | collective-permute-start | bytes 294920 | tf_op jit(solution)/shard_map/ppermute | solution.py:377
  118.6 4.5 %collective-permute-start.23 = (f32[16,128]{1,0:T(8,128)S(1)}, f32[16,128]{1,0:T(8,128)S(1)}, u32[]{:S(2)}, u32[]{:S(2)}) collective-permute-start(f32[16,128]{1,0:T(8,128)S(1)} %add.127), channel_id=1, source_target_pairs={{0,16},{2,18},{4,20},{6,22},{8,24},{10,26},{12,28},{14,30},{16,0},... | collective-permute-start | bytes 24584 | tf_op jit(solution)/shard_map/ppermute | solution.py:377
  123.2 3.7 %collective-permute-start.24 = (f32[16,128]{1,0:T(8,128)S(1)}, f32[16,128]{1,0:T(8,128)S(1)}, u32[]{:S(2)}, u32[]{:S(2)}) collective-permute-start(f32[16,128]{1,0:T(8,128)S(1)} %add.132.refs_0_), channel_id=1, source_target_pairs={{0,1},{1,0},{2,3},{3,2},{4,5},{5,4},{6,7},{7,6},{8,9},{9,8},{10,11... | collective-permute-start | bytes 24584 | tf_op jit(solution)/shard_map/ppermute | solution.py:377
